TPU v7x, 128 devices: a whole 4x4x4 slice. The times are simulated.
128 devices in a mesh: dp: 1, yax: 16 (over z, y), xax: 8 (over x, core).
Axes of the slice: x: 4, y: 4, z: 4, core: 2. Of those that a mesh axis runs over, the one named last changes fastest.
Arguments:
- hidden: bfloat16 [768, 4096], P('dp', 'xax')
- cache_len: int32 [768], P('dp')
- k_cache: bfloat16 [768, 1024, 128], P(('dp', 'yax', 'xax'))
- v_cache: bfloat16 [768, 1024, 128], P(('dp', 'yax', 'xax'))
- g_attn: float32 [4096], P('xax')
- w_query: bfloat16 [4096, 4096], P('xax', 'yax')
- w_key: bfloat16 [4096, 128], P('xax')
- w_value: bfloat16 [4096, 128], P('xax')
- w_gate: bfloat16 [4096, 16384], P('xax', 'yax')
- w_up: bfloat16 [4096, 16384], P('xax', 'yax')
- w_out: bfloat16 [4096, 4096], P('yax', 'xax')
- w_down: bfloat16 [16384, 4096], P('yax', 'xax')
- g_final: float32 [4096], P('xax')
- embedding: bfloat16 [50432, 4096], P('yax', 'xax')
Outputs:
- output 1: bfloat16 [768, 128], P(('dp', 'yax', 'xax'))
- output 2: bfloat16 [768, 128], P(('dp', 'yax', 'xax'))
- output 3: float32 [768, 50432], P('dp', ('yax', 'xax'))
- output 4: float32 [768], P('dp')
All inputs are finite; a program needn't handle non-finite values.
Results may differ from a plain program's by a relative error of at most 0.00127.
Values are sent between devices in bfloat16 or wider.
A program may use at most 1 GiB of HBM per device.

v0:
```python
import jax
import jax.numpy as jnp
from jax import lax
from jax.sharding import PartitionSpec as P

EPS = 1e-6
ROPE_BASE = 10000.0


def rope_angle(positions, head_dim):
    half_dim = head_dim // 2
    inv_freq = ROPE_BASE ** (-(jnp.arange(half_dim, dtype=jnp.float32) * 2.0) / head_dim)
    return positions.astype(jnp.float32)[:, None] * inv_freq[None, :]


def rotary(values_in, angles):
    half_dim = values_in.shape[-1] // 2
    cos_a = jnp.cos(angles)
    sin_a = jnp.sin(angles)
    first = values_in[..., :half_dim]
    second = values_in[..., half_dim:]
    return jnp.concatenate([first * cos_a - second * sin_a, second * cos_a + first * sin_a], axis=-1)


def sharded_norm(values_in, gain, width):
    stats = jnp.stack([jnp.sum(values_in, axis=-1), jnp.sum(values_in * values_in, axis=-1)])
    stats = lax.psum(stats, "xax")
    row_mean = stats[0] / width
    row_var = stats[1] / width - row_mean * row_mean
    return (values_in - row_mean[:, None]) * lax.rsqrt(row_var + EPS)[:, None] * gain


def attend_local(query, k_cache, v_cache, key_new, value_new, lengths):
    score_scale = query.shape[-1] ** -0.5
    scores = jnp.einsum("bhe,bse->bhs", query, k_cache, preferred_element_type=jnp.float32) * score_scale
    score_new = jnp.einsum("bhe,be->bh", query, key_new, preferred_element_type=jnp.float32) * score_scale
    valid = jnp.arange(k_cache.shape[1])[None, None, :] < lengths[:, None, None]
    row_max = jnp.maximum(jnp.max(jnp.where(valid, scores, -jnp.inf), axis=-1), score_new)
    weights = jnp.where(valid, jnp.exp(scores - row_max[..., None]), 0.0)
    weight_new = jnp.exp(score_new - row_max)
    denominator = jnp.sum(weights, axis=-1) + weight_new
    prob_all = (weights / denominator[..., None]).astype(jnp.bfloat16)
    prob_new = (weight_new / denominator).astype(jnp.bfloat16)
    attn_out = jnp.einsum("bhs,bse->bhe", prob_all, v_cache, preferred_element_type=jnp.float32)
    attn_out = attn_out + prob_new.astype(jnp.float32)[..., None] * value_new.astype(jnp.float32)[:, None, :]
    return attn_out.astype(jnp.bfloat16)


def solution(mesh):
    y_size = mesh.shape["yax"]
    x_size = mesh.shape["xax"]
    row_spec = P(("dp", "yax", "xax"))

    def local_step(hidden, cache_len, k_cache, v_cache, g_attn, w_query, w_key, w_value,
                   w_gate, w_up, w_out, w_down, g_final, embedding):
        rows = hidden.shape[0]
        width = hidden.shape[1] * x_size
        own_rows = k_cache.shape[0]
        head_dim = k_cache.shape[2]
        q_cols = w_query.shape[1]
        kv_end = q_cols + 2 * head_dim
        ff_end = kv_end + w_gate.shape[1]
        y_idx = lax.axis_index("yax")
        x_idx = lax.axis_index("xax")
        own_start = (y_idx * x_size + x_idx) * own_rows

        residual = hidden.astype(jnp.float32)
        normed = sharded_norm(residual, g_attn, width).astype(jnp.bfloat16)
        proj_part = jnp.concatenate([
            jnp.dot(normed, w_query, preferred_element_type=jnp.float32),
            jnp.dot(normed, w_key, preferred_element_type=jnp.float32),
            jnp.dot(normed, w_value, preferred_element_type=jnp.float32),
            jnp.dot(normed, w_gate, preferred_element_type=jnp.float32),
            jnp.dot(normed, w_up, preferred_element_type=jnp.float32)], axis=1)
        projected = lax.psum(proj_part, "xax").astype(jnp.bfloat16)
        angles = rope_angle(cache_len, head_dim)
        query = projected[:, :q_cols].astype(jnp.float32).reshape(rows, q_cols // head_dim, head_dim)
        query = rotary(query, angles[:, None, :]).astype(jnp.bfloat16)
        key_new = rotary(projected[:, q_cols:q_cols + head_dim].astype(jnp.float32), angles).astype(jnp.bfloat16)
        value_new = projected[:, q_cols + head_dim:kv_end]
        gate = projected[:, kv_end:ff_end]
        up_val = projected[:, ff_end:]

        query_grp = lax.all_to_all(query, "yax", 0, 1, tiled=True)
        query_own = lax.dynamic_slice_in_dim(query_grp, x_idx * own_rows, own_rows, axis=0)
        key_own = lax.dynamic_slice_in_dim(key_new, own_start, own_rows, axis=0)
        value_own = lax.dynamic_slice_in_dim(value_new, own_start, own_rows, axis=0)
        len_own = lax.dynamic_slice_in_dim(cache_len, own_start, own_rows, axis=0)
        attn_own = attend_local(query_own, k_cache, v_cache, key_own, value_own, len_own)
        attn_grp = lax.all_gather(attn_own, "xax", axis=0, tiled=True)
        attn_heads = lax.all_to_all(attn_grp, "yax", 1, 0, tiled=True).reshape(rows, q_cols)

        mlp_act = (jax.nn.silu(gate.astype(jnp.float32)) * up_val.astype(jnp.float32)).astype(jnp.bfloat16)
        branch_sum = (jnp.dot(attn_heads, w_out, preferred_element_type=jnp.float32)
                      + jnp.dot(mlp_act, w_down, preferred_element_type=jnp.float32))
        residual_out = residual + lax.psum(branch_sum, "yax")
        final_norm = sharded_norm(residual_out, g_final, width).astype(jnp.bfloat16)
        logit_part = jnp.einsum("bd,vd->bv", final_norm, embedding, preferred_element_type=jnp.float32)
        logits = lax.psum_scatter(logit_part, "xax", scatter_dimension=1, tiled=True)
        row_max = lax.pmax(jnp.max(logits, axis=1), ("yax", "xax"))
        sum_exp = lax.psum(jnp.sum(jnp.exp(logits - row_max[:, None]), axis=1), ("yax", "xax"))
        log_norm = row_max + jnp.log(sum_exp)
        return key_own, value_own, logits - log_norm[:, None], log_norm

    in_specs = (P("dp", "xax"), P("dp"), row_spec, row_spec, P("xax"), P("xax", "yax"),
                P("xax", None), P("xax", None), P("xax", "yax"), P("xax", "yax"),
                P("yax", "xax"), P("yax", "xax"), P("xax"), P("yax", "xax"))
    out_specs = (row_spec, row_spec, P("dp", ("yax", "xax")), P("dp"))
    return jax.shard_map(local_step, mesh=mesh, in_specs=in_specs, out_specs=out_specs, check_vma=False)
```

profile of v0, /device:TPU:1, one launch (start us, length us, event | category | flops | bytes accessed | tf_op | source)
XLA Modules:
  0.0 505.3 jit_solution(5225230697751499290)
XLA Ops:
  7.2 0.0 copy-start
  7.2 1.6 convert_reduce_fusion
  8.8 0.0 copy-start.14
  8.8 13.4 %psum.35 = f32[2,768]{1,0:T(2,128)S(1)} all-reduce(f32[2,768]{1,0:T(2,128)S(1)} %pad_maximum_fusion.1), channel_id=1, replica_groups=mesh['dp'=1,'yax'=16,'xax'=8] {'xax'}, use_global_device_ids=true, to_apply=%region_2.0 | all-reduce | flops 1536 | bytes 12288 | tf_op jit(solution)/shard_map/psum | solution.py:27
  22.2 0.0 copy-start.1
  22.3 2.7 convolution_dynamic-update-slice_fusion.2
  25.0 0.0 copy-done.12
  25.0 0.0 copy-done.14
  25.0 0.0 copy-done.1
  25.0 0.0 copy-start.13
  25.0 1.2 convolution_dynamic-update-slice_fusion.4
  26.3 0.0 copy-done.13
  26.3 1.3 convolution_dynamic-update-slice_fusion.3
  27.6 0.0 copy-done.10
  27.6 2.8 convolution_dynamic-update-slice_fusion.1
  30.5 0.0 copy-done.11
  30.5 2.8 convolution_dynamic-update-slice_fusion
  33.3 87.1 %all-reduce.6 = bf16[768,2560]{1,0:T(8,128)(2,1)} all-reduce(f32[768,2560]{1,0:T(8,128)} %convolution_dynamic-update-slice_fusion), channel_id=1, replica_groups=mesh['dp'=1,'yax'=16,'xax'=8] {'xax'}, use_global_device_ids=true, to_apply=%region_3.0 | all-reduce | flops 1966080 | bytes 11796480 | tf_op jit(solution)/shard_map/psum | solution.py:75
  120.4 1.9 fusion.49
  122.3 1.9 slice_convert_fusion
  124.2 0.0 copy-done.7
  124.2 2.4 reshape.146
  126.6 3.8 multiply_cosine_fusion
  130.4 0.0 copy-done.2
  130.4 1.4 subtract_convert_fusion
  131.8 1.8 pad_maximum_fusion
  133.6 7.8 %all-to-all-start = ((bf16[768,2,128]{2,1,0:T(2,128)(2,1)}), bf16[768,2,128]{2,1,0:T(2,128)(2,1)}, u32[]{:S(2)}, u32[]{:S(2)}) async-start(bf16[768,2,128]{2,1,0:T(2,128)(2,1)} %pad_maximum_fusion), calls=%async_computation | async-start | bytes 786432 | tf_op jit(solution)/shard_map/all_to_all | solution.py:84
  141.4 0.8 fusion.36
  142.2 0.1 dynamic_slice.14
  142.3 1.3 fusion.48
  143.5 0.1 iota_compare_fusion
  143.6 5.9 %all-to-all-done = bf16[768,2,128]{2,1,0:T(2,128)(2,1)} async-done(((bf16[768,2,128]{2,1,0:T(2,128)(2,1)}), bf16[768,2,128]{2,1,0:T(2,128)(2,1)}, u32[]{:S(2)}, u32[]{:S(2)}) %all-to-all-start) | async-done | bytes 393248 | tf_op jit(solution)/shard_map/all_to_all | solution.py:84
  149.5 1.3 copy.30
  150.8 0.1 fusion.25
  150.9 2.3 select_reduce_fusion
  153.2 0.3 fusion.17
  153.5 0.5 fusion.12
  154.0 15.5 %all_gather.3 = bf16[48,32,128]{2,1,0:T(8,128)(2,1)S(1)} all-gather(bf16[6,32,128]{2,1,0:T(8,128)(2,1)S(1)} %fusion.12), channel_id=1, replica_groups=mesh['dp'=1,'yax'=16,'xax'=8] {'xax'}, dimensions={0}, use_global_device_ids=true | all-gather | bytes 442368 | tf_op jit(solution)/shard_map/all_gather | solution.py:90
  169.5 0.9 copy.31
  170.4 4.2 all-to-all-start.1
  174.6 0.0 copy-start.3
  174.6 0.2 all-reduce.5.cloned.1.call-start
  174.9 4.4 fusion.10
  179.3 5.0 all-to-all-done.1
  184.3 1.3 copy.32
  185.6 2.9 convolution_add_fusion
  188.5 0.0 all-reduce.5.cloned.1.call-update
  188.5 0.0 copy-start.4
  188.5 83.5 %all-reduce.5.cloned.1.call-done = f32[768,512]{1,0:T(8,128)} async-done(((f32[768,512]{1,0:T(8,128)}), f32[768,512]{1,0:T(8,128)}) %all-reduce.5.cloned.1.call-update) | async-done | bytes 1572880 | tf_op jit(solution)/shard_map/psum | solution.py:96
  272.0 1.9 fusion.18
  274.0 14.2 %psum.38 = f32[2,768]{1,0:T(2,128)S(1)} all-reduce(f32[2,768]{1,0:T(2,128)S(1)} %pad_maximum_fusion.2), channel_id=1, replica_groups=mesh['dp'=1,'yax'=16,'xax'=8] {'xax'}, use_global_device_ids=true, to_apply=%region_9.10 | all-reduce | flops 1536 | bytes 12288 | tf_op jit(solution)/shard_map/psum | solution.py:27
  288.2 7.0 %fusion.13 = f32[768,3152]{0,1:T(8,128)} fusion(bf16[3152,512]{1,0:T(8,128)(2,1)S(1)} %copy-done, f32[512]{0:T(512)S(1)} %copy-done.4, f32[768]{0:T(1024)S(1)} %add_rsqrt_fusion, f32[768]{0:T(1024)S(1)} %get-tuple-element.8, f32[768,512]{1,0:T(8,128)} %all-reduce.5.cloned.1.call-done, bf16[768,512]{1,0:T(8,128)(2,1)} %param.14), kind=kOutput, calls=%fused_computation.30 | convolution fusion | flops 2481192960 | bytes 15278080 | tf_op jit(solution)/shard_map/bd,vd->bv/dot_general | solution.py:98
  295.2 58.8 %fusion = f32[768,400]{0,1:T(8,128)} fusion(f32[768,3152]{0,1:T(8,128)} %fusion.13), kind=kCustom, calls=%all-reduce-scatter | all-reduce-scatter fusion | flops 2457601 | bytes 10912256
  354.0 0.9 slice.65
  355.0 4.4 collective-permute-start
  359.4 0.6 dynamic-slice.4
  360.6 0.8 collective-permute-done
  361.5 5.2 %concatenate.14 = f32[768,442]{0,1:T(8,128)} concatenate(f32[768,42]{0,1:T(8,128)S(1)} %collective-permute-done, f32[768,400]{0,1:T(8,128)} %fusion), dimensions={1} | concatenate | bytes 2715648
  366.7 1.5 dynamic-slice_reduce_fusion
  368.1 63.7 %pmax.7 = f32[768]{0:T(1024)S(1)} all-reduce(f32[768]{0:T(1024)S(1)} %dynamic-slice_reduce_fusion), channel_id=1, replica_groups=mesh['dp'=1,'yax'=16,'xax'=8] {'yax','xax'}, use_global_device_ids=true, to_apply=%region_12.13 | all-reduce | flops 768 | bytes 6144 | tf_op jit(solution)/shard_map/pmax | solution.py:100
  431.8 1.6 exponential_reduce_fusion
  433.3 62.6 %psum.39 = f32[768]{0:T(1024)S(1)} all-reduce(f32[768]{0:T(1024)S(1)} %exponential_reduce_fusion), channel_id=1, replica_groups=mesh['dp'=1,'yax'=16,'xax'=8] {'yax','xax'}, use_global_device_ids=true, to_apply=%region_14.15 | all-reduce | flops 768 | bytes 6144 | tf_op jit(solution)/shard_map/psum | solution.py:101
  496.0 2.5 dynamic-slice_subtract_fusion
  498.4 0.0 copy-done.5
  (30 shorter events, 0.2 us)
Async XLA Ops:
  7.2 281.1 %copy-start = (bf16[3152,512]{1,0:T(8,128)(2,1)S(1)}, bf16[3152,512]{1,0:T(8,128)(2,1)}, u32[]{:S(2)}) copy-start(bf16[3152,512]{1,0:T(8,128)(2,1)} %param.27) | copy-start | bytes 9682948
  8.8 16.2 %copy-start.12 = (bf16[512,128]{1,0:T(8,128)(2,1)S(1)}, bf16[512,128]{1,0:T(8,128)(2,1)}, u32[]{:S(2)}) copy-start(bf16[512,128]{1,0:T(8,128)(2,1)} %param.20) | copy-start | bytes 393220
  8.8 16.2 %copy-start.14 = (f32[512]{0:T(512)S(1)}, f32[512]{0:T(512)}, u32[]{:S(2)}) copy-start(f32[512]{0:T(512)} %param.18) | copy-start | bytes 6148
  22.2 2.8 copy-start.1
  25.0 1.3 copy-start.13
  26.3 1.4 copy-start.10
  27.6 2.8 copy-start.11
  120.4 3.8 copy-start.7
  126.6 3.8 copy-start.2
  133.6 15.9 %all-to-all-start = ((bf16[768,2,128]{2,1,0:T(2,128)(2,1)}), bf16[768,2,128]{2,1,0:T(2,128)(2,1)}, u32[]{:S(2)}, u32[]{:S(2)}) async-start(bf16[768,2,128]{2,1,0:T(2,128)(2,1)} %pad_maximum_fusion), calls=%async_computation | async-start | bytes 786432 | tf_op jit(solution)/shard_map/all_to_all | solution.py:84
  142.2 11.0 %copy-start.6 = (bf16[6,128]{1,0:T(8,128)(2,1)}, bf16[6,128]{1,0:T(8,128)(2,1)S(1)}, u32[]{:S(2)}) copy-start(bf16[6,128]{1,0:T(8,128)(2,1)S(1)} %fusion.36) | copy-start | bytes 4612
  150.9 2.6 copy-start.9
  170.4 13.9 %all-to-all-start.1 = ((bf16[48,32,128]{2,0,1:T(8,128)(2,1)}), bf16[48,32,128]{2,0,1:T(8,128)(2,1)}, u32[]{:S(2)}, u32[]{:S(2)}) async-start(bf16[48,32,128]{2,0,1:T(8,128)(2,1)} %copy.31), calls=%async_computation.1 | async-start | bytes 786432 | tf_op jit(solution)/shard_map/all_to_all | solution.py:91
  174.6 11.0 %copy-start.3 = (bf16[256,512]{1,0:T(8,128)(2,1)S(1)}, bf16[256,512]{1,0:T(8,128)(2,1)}, u32[]{:S(2)}) copy-start(bf16[256,512]{1,0:T(8,128)(2,1)} %param.24) | copy-start | bytes 786436
  174.6 97.4 %all-reduce.5.cloned.1.call-start = ((), (), s32[]{:S(2)}) async-start(), calls=%async_computation.2 | async-start | bytes 3145728 | tf_op jit(solution)/shard_map/psum | solution.py:96
  188.5 99.7 %copy-start.4 = (f32[512]{0:T(512)S(1)}, f32[512]{0:T(512)}, u32[]{:S(2)}) copy-start(f32[512]{0:T(512)} %param.26) | copy-start | bytes 6148
  295.2 64.2 %copy-start.8 = (u32[128]{0:T(128)S(1)}, u32[128]{0:T(128)}, u32[]{:S(2)}) copy-start(u32[128]{0:T(128)} %constant.48) | copy-start | bytes 1540
  355.0 6.5 %collective-permute-start = (f32[768,42]{0,1:T(8,128)S(1)}, f32[768,42]{0,1:T(8,128)S(1)}, u32[]{:S(2)}, u32[]{:S(2)}) collective-permute-start(f32[768,42]{0,1:T(8,128)S(1)} %slice.65), channel_id=1, source_target_pairs={{0,1},{1,2},{2,3},{3,4},{4,5},{5,6},{6,7},{8,9},{9,10},{10,11},{11... | collective-permute-start | bytes 387080
  496.0 2.5 copy-start.5
Sparse Core Ops, SparseCore 0:
  188.6 83.3 all-reduce.4
where the time goes:
time: 506 us; the launch traced here: 505 us
  blocking collectives  315 us (62%)
  waiting for transfers between devices  95.2 us (19%)
  matrix products  28.1 us (6%)
  other arithmetic  22.3 us (4%)
  starting transfers between devices  16.6 us (3%)
  between operations  15 us (3%)
  local copies, waits for them, and re-layouts  12.7 us (3%)
    psum x1, blocking collectives, local_step(): projected = lax.psum(proj_part, 'xax').astype(jnp.bfloat16)  87.1 us
    psum x1, waiting for transfers between devices, local_step(): residual_out = residual + lax.psum(branch_sum, 'yax')  83.5 us
    pmax x1, blocking collectives, local_step(): row_max = lax.pmax(jnp.max(logits, axis=1), ('yax', 'xax'))  63.7 us
    psum x1, blocking collectives, local_step(): lax.psum(jnp.sum(jnp.exp(logits - row_max[:, None]), axis=1), ('yax', 'xa...  62.6 us
    unnamed x1, blocking collectives  58.8 us
    psum x2, blocking collectives, sharded_norm(): stats = lax.psum(stats, 'xax')  27.6 us
    all_gather x1, blocking collectives, local_step(): attn_grp = lax.all_gather(attn_own, 'xax', axis=0, tiled=True)  15.5 us
  transfers between devices with their start and end apart: 4, of which 4 were waited for; matrix products, arithmetic and copies ran while one was open for 1% of the time, Pallas kernels for 0%

commit v1 on v0

--- a/solution.py
+++ b/solution.py
@@ -1,10 +1,14 @@
 import jax
 import jax.numpy as jnp
 from jax import lax
+from jax.experimental import pallas as pl
+from jax.experimental.pallas import tpu as pltpu
 from jax.sharding import PartitionSpec as P
 
 EPS = 1e-6
 ROPE_BASE = 10000.0
+MESH_ID = pl.DeviceIdType.MESH
+NY, NZ, NX = 4, 4, 4
 
 
 def rope_angle(positions, head_dim):
@@ -44,6 +48,281 @@
     attn_out = jnp.einsum("bhs,bse->bhe", prob_all, v_cache, preferred_element_type=jnp.float32)
     attn_out = attn_out + prob_new.astype(jnp.float32)[..., None] * value_new.astype(jnp.float32)[:, None, :]
     return attn_out.astype(jnp.bfloat16)
+
+
+class Links:
+    def __init__(self, send_sem, recv_sem):
+        self.send_sem, self.recv_sem, self.count, self.sent = send_sem, recv_sem, 0, []
+        self.y_idx = lax.axis_index("yax")
+        self.x_idx = lax.axis_index("xax")
+        self.z, self.y = self.y_idx // NY, self.y_idx % NY
+        self.chip, self.core = self.x_idx // 2, self.x_idx % 2
+
+    def at_plane(self, dz, dy):
+        return {"yax": (self.z + dz) % NZ * NY + (self.y + dy) % NY, "xax": self.x_idx}
+
+    def at_line(self, dx, other_core):
+        core = 1 - self.core if other_core else self.core
+        return {"yax": self.y_idx, "xax": (self.chip + dx) % NX * 2 + core}
+
+    def send(self, src, dst, where):
+        copy = pltpu.make_async_remote_copy(
+            src_ref=src, dst_ref=dst, send_sem=self.send_sem.at[self.count], recv_sem=self.recv_sem.at[self.count],
+            device_id=where, device_id_type=MESH_ID)
+        self.count += 1
+        copy.start()
+        self.sent.append(copy)
+        return copy
+
+    def finish(self):
+        for copy in self.sent:
+            copy.wait_send()
+        self.sent = []
+
+    def barrier(self):
+        barrier = pltpu.get_barrier_semaphore()
+        peers = [self.at_line(dx, oc) for dx in range(NX) for oc in (0, 1) if (dx, oc) != (0, 0)]
+        peers += [self.at_plane(dz, dy) for dz in range(NZ) for dy in range(NY) if (dz, dy) != (0, 0)]
+        for peer in peers:
+            pl.semaphore_signal(barrier, inc=1, device_id=peer, device_id_type=MESH_ID)
+        pl.semaphore_wait(barrier, len(peers))
+
+
+def plane_gather(links, buf):
+    cols = buf.shape[-1]
+    parts = []
+    for part in range(2):
+        lo = part * (cols // 2)
+        mid = lo + cols // 4
+        hi = lo + cols // 2
+
+        def slot(du, dv, a, b, half=0, part=part):
+            dz, dy = (dv, du) if part == 0 else (du, dv)
+            return buf.at[half, (links.z + dz) % NZ, (links.y + dy) % NY, :, pl.ds(a, b - a)]
+
+        def node(du, dv, part=part):
+            return links.at_plane(dv, du) if part == 0 else links.at_plane(du, dv)
+
+        parts.append((lo, mid, hi, slot, node))
+
+    partner = links.at_line(0, True)
+    crossing = []
+
+    def give(p, du, dv):
+        lo, mid, hi, slot, node = p
+        crossing.append(links.send(slot(du, dv, lo, hi), slot(du, dv, lo, hi, half=1), partner))
+
+    def push(p, du, dv, to_u, to_v, a=None, b=None):
+        lo, mid, hi, slot, node = p
+        a, b = (lo if a is None else a), (hi if b is None else b)
+        return links.send(slot(du, dv, a, b), slot(du, dv, a, b), node(to_u, to_v))
+
+    state = []
+    for p in parts:
+        s = {"u+": push(p, 0, 0, 1, 0), "u-": push(p, 0, 0, -1, 0)}
+        s["v+", 0] = push(p, 0, 0, 0, 1)
+        s["v-", 0] = push(p, 0, 0, 0, -1)
+        state.append(s)
+    for p in parts:
+        give(p, 0, 0)
+    for p, s in zip(parts, state):
+        s["u+"].wait_recv()
+        s["ur+"] = push(p, -1, 0, 1, 0, p[0], p[1])
+        s["v+", 1] = push(p, -1, 0, 0, 1)
+        s["v-", 1] = push(p, -1, 0, 0, -1)
+        give(p, -1, 0)
+    for p, s in zip(parts, state):
+        s["u-"].wait_recv()
+        s["ur-"] = push(p, 1, 0, -1, 0, p[1], p[2])
+        s["v+", 2] = push(p, 1, 0, 0, 1)
+        s["v-", 2] = push(p, 1, 0, 0, -1)
+        give(p, 1, 0)
+    offset = {0: 0, 1: -1, 2: 1, 3: 2}
+
+    def arrive(p, s, k):
+        s["v+", k].wait_recv()
+        if k in (0, 3):
+            s["vr+", k] = push(p, offset[k], -1, 0, 1)
+        give(p, offset[k], -1)
+        s["v-", k].wait_recv()
+        if k in (1, 2):
+            s["vr-", k] = push(p, offset[k], 1, 0, -1)
+        give(p, offset[k], 1)
+
+    for p, s in zip(parts, state):
+        arrive(p, s, 0)
+    for p, s in zip(parts, state):
+        s["ur+"].wait_recv()
+        s["ur-"].wait_recv()
+        s["v+", 3] = push(p, 2, 0, 0, 1)
+        s["v-", 3] = push(p, 2, 0, 0, -1)
+        give(p, 2, 0)
+    for k in (1, 2, 3):
+        for p, s in zip(parts, state):
+            arrive(p, s, k)
+    for k, name in ((0, "vr+"), (1, "vr-"), (2, "vr-"), (3, "vr+")):
+        for p, s in zip(parts, state):
+            s[name, k].wait_recv()
+            give(p, offset[k], 2)
+    return crossing
+
+
+def eye_mask():
+    return lax.broadcasted_iota(jnp.int32, (128, 128), 0) == lax.broadcasted_iota(jnp.int32, (128, 128), 1)
+
+
+def tail_kernel(vocab_own, part_ref, hid_ref, gain_ref, emb_ref, z_ref, norm_ref,
+                ra1, rb1, ra2, rb2, acc_a, acc_b, xbuf, stat, f_buf, emb_buf, lse_x, lse_y,
+                send_sem, recv_sem, local_sem):
+    links = Links(send_sem, recv_sem)
+    z, y = links.z, links.y
+    half = part_ref.shape[-1] // 2
+    rows = part_ref.shape[2]
+    chunk = part_ref.shape[-1]
+    take = emb_buf.shape[1]
+    align = 16
+
+    def emb_start(xid):
+        first = vocab_own * xid // align * align
+        return pl.multiple_of(first - xid // (2 * NX - 1) * align, align)
+
+    def emb_piece(dx, other):
+        core = 1 - links.core if other else links.core
+        xid = (links.chip + dx) % NX * 2 + core
+        return emb_ref.at[pl.ds(emb_start(xid), take), :]
+
+    def emb_slot(dx, other):
+        back = (NX - dx) % NX
+        return emb_buf.at[int(other), :, pl.ds(back * chunk, chunk)]
+
+    local = pltpu.make_async_copy(emb_piece(0, 0), emb_slot(0, 0), local_sem)
+    local.start()
+    links.barrier()
+
+    low, high = pl.ds(0, half), pl.ds(half, half)
+    first = []
+    for d in (1, 3, 2):
+        first.append((
+            links.send(part_ref.at[:, (y + d) % NY, :, low], ra1.at[d - 1], links.at_plane(0, d)),
+            links.send(part_ref.at[(z + d) % NZ, :, :, high], rb1.at[d - 1], links.at_plane(d, 0))))
+    emb = [links.send(emb_piece(dx, oc), emb_slot(dx, oc), links.at_line(dx, oc))
+           for dx, oc in ((0, 1), (1, 0), (3, 0), (1, 1), (3, 1))]
+    for ca, cb in first:
+        ca.wait_recv()
+        cb.wait_recv()
+    acc_a[...] = (part_ref[:, y, :, :half] + ra1[0]) + (ra1[1] + ra1[2])
+    second_a = [links.send(acc_a.at[(z + d) % NZ], ra2.at[d - 1], links.at_plane(d, 0)) for d in (1, 3, 2)]
+    acc_b[...] = (part_ref[z, :, :, half:] + rb1[0]) + (rb1[1] + rb1[2])
+    second_b = [links.send(acc_b.at[(y + d) % NY], rb2.at[d - 1], links.at_plane(0, d)) for d in (1, 3, 2)]
+    for c in second_a + second_b:
+        c.wait_recv()
+    res = hid_ref[z, y].astype(jnp.float32)
+    xbuf[0, :rows, :half] = res[:, :half] + ((acc_a[z] + ra2[0]) + (ra2[1] + ra2[2]))
+    xbuf[0, :rows, half:] = res[:, half:] + ((acc_b[y] + rb2[0]) + (rb2[1] + rb2[2]))
+    xbuf[0, rows:, :] = jnp.broadcast_to(gain_ref[...], (8, chunk))
+
+    line = [links.send(xbuf.at[0], xbuf.at[(NX - dx) % NX], links.at_line(dx, 0)) for dx in (1, 3, 2)]
+    emb += [links.send(emb_piece(2, oc), emb_slot(2, oc), links.at_line(2, oc)) for oc in (0, 1)]
+    for c in line:
+        c.wait_recv()
+    held = xbuf[:, :rows, :]
+    count = NX * chunk
+    mean = jnp.sum(jnp.sum(held, axis=0), axis=-1, keepdims=True) / count
+    dev = held - mean[None]
+    square = jnp.sum(jnp.sum(dev * dev, axis=0), axis=-1, keepdims=True)
+    lane = lax.broadcasted_iota(jnp.int32, (rows, 128), 1)
+    stat[0] = jnp.where(lane == 0, mean, square)
+    links.send(stat.at[0], stat.at[1], links.at_line(0, True)).wait_recv()
+    other_mean, other_square = stat[1, :, 0:1], stat[1, :, 1:2]
+    both = (mean + other_mean) * 0.5
+    gap = mean - other_mean
+    var = (square + other_square + gap * gap * (count * 0.5)) / (2 * count)
+    scale = lax.rsqrt(var + EPS)
+    for e in range(NX):
+        f_buf[0, z, y, :, e * chunk:(e + 1) * chunk] = (
+            (xbuf[e, :rows, :] - both) * scale * xbuf[e, rows:rows + 1, :]).astype(jnp.bfloat16)
+
+    crossing = plane_gather(links, f_buf)
+    local.wait()
+    for c in emb:
+        c.wait_recv()
+    for c in crossing:
+        c.wait_recv()
+
+    group = NY * rows
+    for i in range(NZ):
+        total = None
+        for h in range(2):
+            term = lax.dot_general(f_buf[h, i].reshape(group, NX * chunk), emb_buf[h],
+                                   (((1,), (1,)), ((), ())), preferred_element_type=jnp.float32)
+            total = term if total is None else total + term
+        z_ref[i * group:(i + 1) * group, :] = total
+
+    xid = links.x_idx
+    shift = vocab_own * xid - emb_start(xid)
+    eye = eye_mask()
+    col = lax.broadcasted_iota(jnp.int32, (128, take), 1)
+    own = (col >= shift) & (col < shift + vocab_own)
+    blocks = z_ref.shape[0] // 128
+    for b in range(blocks):
+        zb = jnp.where(own, z_ref[b * 128:(b + 1) * 128, :], -jnp.inf)
+        top = jnp.max(zb, axis=1, keepdims=True)
+        mass = jnp.sum(jnp.exp(zb - top), axis=1, keepdims=True)
+        lse_x[xid, b:b + 1, :] = jnp.sum(jnp.where(eye, top, 0.0), axis=0, keepdims=True)
+        lse_x[xid, 8 + b:9 + b, :] = jnp.sum(jnp.where(eye, mass, 0.0), axis=0, keepdims=True)
+    for b in range(blocks, 8):
+        lse_x[xid, b:b + 1, :] = jnp.zeros((1, 128), jnp.float32)
+        lse_x[xid, 8 + b:9 + b, :] = jnp.ones((1, 128), jnp.float32)
+
+    def merge(ref):
+        tops = ref[:, :8, :]
+        top = jnp.max(tops, axis=0)
+        return top, jnp.sum(ref[:, 8:, :] * jnp.exp(tops - top[None]), axis=0)
+
+    got = [links.send(lse_x.at[xid], lse_x.at[xid], links.at_line(dx, oc))
+           for dx in range(NX) for oc in (0, 1) if (dx, oc) != (0, 0)]
+    for c in got:
+        c.wait_recv()
+    top, mass = merge(lse_x)
+    yid = links.y_idx
+    lse_y[yid, :8, :] = top
+    lse_y[yid, 8:, :] = mass
+    got = [links.send(lse_y.at[yid], lse_y.at[yid], links.at_plane(dz, dy))
+           for dz in range(NZ) for dy in range(NY) if (dz, dy) != (0, 0)]
+    for c in got:
+        c.wait_recv()
+    top, mass = merge(lse_y)
+    norm_ref[...] = top + jnp.log(mass)
+    links.finish()
+
+
+def tail(part, hidden, g_final, embedding, vocab_own):
+    total_rows, chunk = part.shape
+    rows = total_rows // (NY * NZ)
+    take = (vocab_own + 15 + 15) // 16 * 16
+    half = chunk // 2
+    f32, bf16 = jnp.float32, jnp.bfloat16
+    copies = 100
+    vmem = pl.BlockSpec(memory_space=pltpu.VMEM)
+    hbm = pl.BlockSpec(memory_space=pl.ANY)
+    return pl.pallas_call(
+        lambda *refs: tail_kernel(vocab_own, *refs),
+        out_shape=(jax.ShapeDtypeStruct((total_rows, take), f32), jax.ShapeDtypeStruct((8, 128), f32)),
+        in_specs=[vmem, vmem, vmem, hbm],
+        out_specs=(vmem, vmem),
+        scratch_shapes=[
+            pltpu.VMEM((3, NZ, rows, half), f32), pltpu.VMEM((3, NY, rows, half), f32),
+            pltpu.VMEM((3, rows, half), f32), pltpu.VMEM((3, rows, half), f32),
+            pltpu.VMEM((NZ, rows, half), f32), pltpu.VMEM((NY, rows, half), f32),
+            pltpu.VMEM((NX, rows + 8, chunk), f32), pltpu.VMEM((2, rows, 128), f32),
+            pltpu.VMEM((2, NZ, NY, rows, NX * chunk), bf16), pltpu.VMEM((2, take, NX * chunk), bf16),
+            pltpu.VMEM((2 * NX, 16, 128), f32), pltpu.VMEM((NY * NZ, 16, 128), f32),
+            pltpu.SemaphoreType.DMA((copies + 30,)), pltpu.SemaphoreType.DMA((copies + 30,)), pltpu.SemaphoreType.DMA,
+        ],
+        compiler_params=pltpu.CompilerParams(
+            collective_id=1, has_side_effects=True, vmem_limit_bytes=56 * 1024 * 1024),
+        name="tail",
+    )(part.reshape(NZ, NY, rows, chunk), hidden.reshape(NZ, NY, rows, chunk), g_final[None, :], embedding)
 
 
 def solution(mesh):
@@ -93,13 +372,12 @@
         mlp_act = (jax.nn.silu(gate.astype(jnp.float32)) * up_val.astype(jnp.float32)).astype(jnp.bfloat16)
         branch_sum = (jnp.dot(attn_heads, w_out, preferred_element_type=jnp.float32)
                       + jnp.dot(mlp_act, w_down, preferred_element_type=jnp.float32))
-        residual_out = residual + lax.psum(branch_sum, "yax")
-        final_norm = sharded_norm(residual_out, g_final, width).astype(jnp.bfloat16)
-        logit_part = jnp.einsum("bd,vd->bv", final_norm, embedding, preferred_element_type=jnp.float32)
-        logits = lax.psum_scatter(logit_part, "xax", scatter_dimension=1, tiled=True)
-        row_max = lax.pmax(jnp.max(logits, axis=1), ("yax", "xax"))
-        sum_exp = lax.psum(jnp.sum(jnp.exp(logits - row_max[:, None]), axis=1), ("yax", "xax"))
-        log_norm = row_max + jnp.log(sum_exp)
+
+        vocab_own = embedding.shape[0] // x_size
+        logits_wide, norm_tile = tail(branch_sum, hidden, g_final, embedding, vocab_own)
+        log_norm = norm_tile[:rows // 128].reshape(rows)
+        shift = vocab_own * x_idx - (vocab_own * x_idx // 16 * 16 - x_idx // (x_size - 1) * 16)
+        logits = lax.dynamic_slice_in_dim(logits_wide, shift, vocab_own, axis=1)
         return key_own, value_own, logits - log_norm[:, None], log_norm
 
     in_specs = (P("dp", "xax"), P("dp"), row_spec, row_spec, P("xax"), P("xax", "yax"),

time: 506 us -> 265 us (0.52)
  blocking collectives: 315 us -> 116 us
  Pallas kernels: 0 us -> 87.3 us
  waiting for transfers between devices: 95.2 us -> 13.3 us
  between operations: 15 us -> 0.87 us
  matrix products: 28.1 us -> 17.6 us
  other arithmetic: 22.3 us -> 13.1 us
  local copies, waits for them, and re-layouts: 12.7 us -> 4.52 us
    pallas_call x0 -> x1, Pallas kernels: none -> 87.3 us  [tail(): pl.pallas_call(lambda *refs: tail_kernel(vocab_own, *refs), out_shape=(ja...]
    psum x1 -> x0, waiting for transfers between devices: 83.5 us -> none  [local_step(): residual_out = residual + lax.psum(branch_sum, 'yax')]
    pmax x1 -> x0, blocking collectives: 63.7 us -> none  [local_step(): row_max = lax.pmax(jnp.max(logits, axis=1), ('yax', 'xax'))]
    psum x1 -> x0, blocking collectives: 62.6 us -> none  [local_step(): lax.psum(jnp.sum(jnp.exp(logits - row_max[:, None]), axis=1), ('yax', 'xa...]
    unnamed x1 -> x0, blocking collectives: 58.8 us -> none
    psum x2 -> x1, blocking collectives: 27.6 us -> 13.5 us  [sharded_norm(): stats = lax.psum(stats, 'xax')]
    dot_general x1 -> x0, matrix products: 6.99 us -> none  [local_step(): jnp.einsum('bd,vd->bv', final_norm, embedding, preferred_element_type=jnp...]
  transfers between devices with their start and end apart: 4 -> 2, of which waited for: 4 -> 2; matrix products, arithmetic and copies ran while one was open for 1% -> 2% of each run, Pallas kernels for 0% -> 0%
where the time goes in v1:
time: 265 us; the launch traced here: 264 us
  blocking collectives  116 us (44%)
  Pallas kernels  87.3 us (33%)
  matrix products  17.6 us (7%)
  waiting for transfers between devices  13.3 us (5%)
  other arithmetic  13.1 us (5%)
  starting transfers between devices  11.7 us (4%)
  local copies, waits for them, and re-layouts  4.52 us (2%)
    pallas_call x1, Pallas kernels, tail(): pl.pallas_call(lambda *refs: tail_kernel(vocab_own, *refs), out_shape=(ja...  87.3 us
    psum x1, blocking collectives, local_step(): projected = lax.psum(proj_part, 'xax').astype(jnp.bfloat16)  87.1 us
    all_gather x1, blocking collectives, local_step(): attn_grp = lax.all_gather(attn_own, 'xax', axis=0, tiled=True)  15.4 us
    psum x1, blocking collectives, sharded_norm(): stats = lax.psum(stats, 'xax')  13.5 us
    all_to_all x1, starting transfers between devices, local_step(): query_grp = lax.all_to_all(query, 'yax', 0, 1, tiled=True)  7.77 us
    all_to_all x1, waiting for transfers between devices, local_step(): query_grp = lax.all_to_all(query, 'yax', 0, 1, tiled=True)  6.75 us
    all_to_all x1, waiting for transfers between devices, local_step(): lax.all_to_all(attn_grp, 'yax', 1, 0, tiled=True).reshape(rows, q_cols)  6.58 us
  transfers between devices with their start and end apart: 2, of which 2 were waited for; matrix products, arithmetic and copies ran while one was open for 2% of the time, Pallas kernels for 0%

profile of v1, /device:TPU:1, one launch (start us, length us, event | category | flops | bytes accessed | tf_op | source)
XLA Modules:
  0.0 264.4 jit_solution(8500094243180956818)
XLA Ops:
  0.6 0.0 copy-start
  0.7 1.5 convert_reduce_fusion
  2.2 0.0 copy-start.1
  2.2 0.0 copy-start.8
  2.2 0.0 copy-start.10
  2.3 13.5 %psum.14 = f32[2,768]{1,0:T(2,128)S(1)} all-reduce(f32[2,768]{1,0:T(2,128)S(1)} %pad_maximum_fusion.1), channel_id=1, replica_groups=mesh['dp'=1,'yax'=16,'xax'=8] {'xax'}, use_global_device_ids=true, to_apply=%region_2.0 | all-reduce | flops 1536 | bytes 12288 | tf_op jit(solution)/shard_map/psum | solution.py:31
  15.9 2.6 convolution_dynamic-update-slice_fusion.2
  18.5 0.0 copy-done.1
  18.5 0.0 copy-done.8
  18.5 0.0 copy-done.10
  18.5 0.0 copy-start.9
  18.5 1.2 convolution_dynamic-update-slice_fusion.4
  19.7 0.0 copy-done.9
  19.7 0.0 copy-start.6
  19.7 1.2 convolution_dynamic-update-slice_fusion.3
  21.0 0.0 copy-done.6
  21.0 0.0 copy-start.7
  21.0 2.7 %convolution_dynamic-update-slice_fusion.1 = f32[768,2560]{1,0:T(8,128)} fusion(f32[768,2560]{1,0:T(8,128)} %convolution_dynamic-update-slice_fusion.3, bf16[512,1024]{1,0:T(8,128)(2,1)S(1)} %copy-done.6, bf16[768,512]{1,0:T(8,128)(2,1)S(1)} %copy-done.1, f32[512]{0:T(512)S(1)} %copy-done.10, f32[768]{0:T(1024)S(1)} %add_rsqrt_fusion, ...), kind=kOutput, calls=%fused_computation.11 | convolution fusion | flops 807272448 | bytes 4988928 | tf_op jit(solution)/shard_map/dot_general | solution.py:352
  23.7 0.0 copy-done.7
  23.7 2.8 %convolution_dynamic-update-slice_fusion = f32[768,2560]{1,0:T(8,128)} fusion(f32[768,2560]{1,0:T(8,128)} %convolution_dynamic-update-slice_fusion.1, bf16[512,1024]{1,0:T(8,128)(2,1)S(1)} %copy-done.7, bf16[768,512]{1,0:T(8,128)(2,1)S(1)} %copy-done.1, f32[512]{0:T(512)S(1)} %copy-done.10, f32[768]{0:T(1024)S(1)} %add_rsqrt_fusion, ...), kind=kOutput, calls=%fused_computation.10 | convolution fusion | flops 807272448 | bytes 4988928 | tf_op jit(solution)/shard_map/dot_general | solution.py:353
  26.5 87.1 %all-reduce.1 = bf16[768,2560]{1,0:T(8,128)(2,1)} all-reduce(f32[768,2560]{1,0:T(8,128)} %convolution_dynamic-update-slice_fusion), channel_id=1, replica_groups=mesh['dp'=1,'yax'=16,'xax'=8] {'xax'}, use_global_device_ids=true, to_apply=%region_3.0 | all-reduce | flops 1966080 | bytes 11796480 | tf_op jit(solution)/shard_map/psum | solution.py:354
  113.6 0.0 copy-start.4
  113.6 1.7 fusion.41
  115.4 1.0 slice_convert_fusion
  116.4 0.0 copy-done.4
  116.4 0.4 reshape.132
  116.8 1.8 multiply_cosine_fusion
  118.7 1.4 subtract_convert_fusion
  120.1 1.8 pad_maximum_fusion
  121.9 7.8 %all-to-all-start = ((bf16[768,2,128]{2,1,0:T(2,128)(2,1)}), bf16[768,2,128]{2,1,0:T(2,128)(2,1)S(1)}, u32[]{:S(2)}, u32[]{:S(2)}) async-start(bf16[768,2,128]{2,1,0:T(2,128)(2,1)} %pad_maximum_fusion), calls=%async_computation | async-start | bytes 786432 | tf_op jit(solution)/shard_map/all_to_all | solution.py:363
  129.7 0.1 fusion.28
  129.8 0.0 copy-start.3
  129.8 0.1 dynamic_slice.17
  129.8 1.3 fusion.40
  131.1 0.1 iota_compare_fusion
  131.2 6.7 %all-to-all-done = bf16[768,2,128]{2,1,0:T(2,128)(2,1)S(1)} async-done(((bf16[768,2,128]{2,1,0:T(2,128)(2,1)}), bf16[768,2,128]{2,1,0:T(2,128)(2,1)S(1)}, u32[]{:S(2)}, u32[]{:S(2)}) %all-to-all-start) | async-done | bytes 393248 | tf_op jit(solution)/shard_map/all_to_all | solution.py:363
  137.9 0.3 copy.32
  138.2 0.1 fusion.19
  138.3 0.0 copy-done
  138.3 0.0 copy-start.5
  138.3 0.7 select_reduce_fusion
  139.0 0.0 copy-done.3
  139.1 0.3 fusion.12
  139.4 0.4 copy-done.5
  139.7 0.4 fusion.11
  140.2 15.4 %all_gather.3 = bf16[48,32,128]{2,1,0:T(8,128)(2,1)S(1)} all-gather(bf16[6,32,128]{2,1,0:T(8,128)(2,1)S(1)} %fusion.11), channel_id=1, replica_groups=mesh['dp'=1,'yax'=16,'xax'=8] {'xax'}, dimensions={0}, use_global_device_ids=true | all-gather | bytes 442368 | tf_op jit(solution)/shard_map/all_gather | solution.py:369
  155.6 0.9 copy.33
  156.5 3.9 %all-to-all-start.1 = ((bf16[48,32,128]{2,0,1:T(8,128)(2,1)}), bf16[48,32,128]{2,0,1:T(8,128)(2,1)S(1)}, u32[]{:S(2)}, u32[]{:S(2)}) async-start(bf16[48,32,128]{2,0,1:T(8,128)(2,1)} %copy.33), calls=%async_computation.1 | async-start | bytes 786432 | tf_op jit(solution)/shard_map/all_to_all | solution.py:370
  160.4 3.2 %fusion.9 = f32[768,512]{1,0:T(8,128)S(1)} fusion(bf16[1024,512]{1,0:T(8,128)(2,1)} %param.25, bf16[768,2560]{1,0:T(8,128)(2,1)} %all-reduce.1), kind=kOutput, calls=%fused_computation.17 | convolution fusion | flops 811597824 | bytes 5767168 | tf_op jit(solution)/shard_map/dot_general | solution.py:374
  163.7 6.6 %all-to-all-done.1 = bf16[48,32,128]{2,0,1:T(8,128)(2,1)S(1)} async-done(((bf16[48,32,128]{2,0,1:T(8,128)(2,1)}), bf16[48,32,128]{2,0,1:T(8,128)(2,1)S(1)}, u32[]{:S(2)}, u32[]{:S(2)}) %all-to-all-start.1) | async-done | bytes 393248 | tf_op jit(solution)/shard_map/all_to_all | solution.py:370
  170.2 0.3 copy.34
  170.5 2.5 convolution_add_fusion
  173.0 87.3 %tail.1 = (f32[768,416]{1,0:T(8,128)}, f32[8,128]{1,0:T(8,128)}) custom-call(f32[4,4,48,512]{3,2,1,0:T(8,128)} %bitcast.44, bf16[4,4,48,512]{3,2,1,0:T(8,128)(2,1)} %bitcast.45, f32[1,512]{1,0:T(1,128)} %bitcast.52, bf16[3152,512]{1,0:T(8,128)(2,1)} %refs_3_.1), custom_call_target="tpu_custom_call" | custom-call | tf_op jit(solution)/shard_map/tail/pallas_call | solution.py:308
  260.3 0.7 slice_bitcast_fusion
  261.0 0.0 copy-start.2
  261.0 2.0 dynamic-slice_subtract_fusion
  263.0 0.0 copy-done.2
  263.0 1.5 copy.35
  (9 shorter events, 0.1 us)
Async XLA Ops:
  0.6 137.7 %copy-start = (bf16[6,1024,128]{2,1,0:T(8,128)(2,1)S(1)}, bf16[6,1024,128]{2,1,0:T(8,128)(2,1)}, u32[]{:S(2)}) copy-start(bf16[6,1024,128]{2,1,0:T(8,128)(2,1)} %param.16) | copy-start | bytes 4718596
  2.2 16.3 %copy-start.1 = (bf16[768,512]{1,0:T(8,128)(2,1)S(1)}, bf16[768,512]{1,0:T(8,128)(2,1)}, u32[]{:S(2)}) copy-start(bf16[768,512]{1,0:T(8,128)(2,1)} %param.14) | copy-start | bytes 2359300
  2.2 16.3 %copy-start.8 = (bf16[512,128]{1,0:T(8,128)(2,1)S(1)}, bf16[512,128]{1,0:T(8,128)(2,1)}, u32[]{:S(2)}) copy-start(bf16[512,128]{1,0:T(8,128)(2,1)} %param.20) | copy-start | bytes 393220
  2.2 16.3 %copy-start.10 = (f32[512]{0:T(512)S(1)}, f32[512]{0:T(512)}, u32[]{:S(2)}) copy-start(f32[512]{0:T(512)} %param.18) | copy-start | bytes 6148
  18.5 1.2 copy-start.9
  19.7 1.2 copy-start.6
  21.0 2.7 %copy-start.7 = (bf16[512,1024]{1,0:T(8,128)(2,1)S(1)}, bf16[512,1024]{1,0:T(8,128)(2,1)}, u32[]{:S(2)}) copy-start(bf16[512,1024]{1,0:T(8,128)(2,1)} %param.23) | copy-start | bytes 3145732
  113.6 2.8 %copy-start.4 = (s32[768]{0:T(1024)S(1)}, s32[768]{0:T(1024)}, u32[]{:S(2)}) copy-start(s32[768]{0:T(1024)} %param.15) | copy-start | bytes 9220
  121.9 16.0 %all-to-all-start = ((bf16[768,2,128]{2,1,0:T(2,128)(2,1)}), bf16[768,2,128]{2,1,0:T(2,128)(2,1)S(1)}, u32[]{:S(2)}, u32[]{:S(2)}) async-start(bf16[768,2,128]{2,1,0:T(2,128)(2,1)} %pad_maximum_fusion), calls=%async_computation | async-start | bytes 786432 | tf_op jit(solution)/shard_map/all_to_all | solution.py:363
  129.8 9.3 %copy-start.3 = (bf16[6,128]{1,0:T(8,128)(2,1)}, bf16[6,128]{1,0:T(8,128)(2,1)S(1)}, u32[]{:S(2)}) copy-start(bf16[6,128]{1,0:T(8,128)(2,1)S(1)} %fusion.28) | copy-start | bytes 4612
  138.3 1.4 copy-start.5
  156.5 13.7 %all-to-all-start.1 = ((bf16[48,32,128]{2,0,1:T(8,128)(2,1)}), bf16[48,32,128]{2,0,1:T(8,128)(2,1)S(1)}, u32[]{:S(2)}, u32[]{:S(2)}) async-start(bf16[48,32,128]{2,0,1:T(8,128)(2,1)} %copy.33), calls=%async_computation.1 | async-start | bytes 786432 | tf_op jit(solution)/shard_map/all_to_all | solution.py:370
  261.0 2.0 copy-start.2

commit v2 on v1

v2 whole, which is shorter than its diff:
```python
import jax
import jax.numpy as jnp
from jax import lax
from jax.experimental import pallas as pl
from jax.experimental.pallas import tpu as pltpu
from jax.sharding import PartitionSpec as P

EPS = 1e-6
ROPE_BASE = 10000.0
MESH_ID = pl.DeviceIdType.MESH
NY, NZ, NX = 4, 4, 4


def rope_angle(positions, head_dim):
    half_dim = head_dim // 2
    inv_freq = ROPE_BASE ** (-(jnp.arange(half_dim, dtype=jnp.float32) * 2.0) / head_dim)
    return positions.astype(jnp.float32)[:, None] * inv_freq[None, :]


class Links:
    def __init__(self, send_sem, recv_sem):
        self.send_sem, self.recv_sem, self.count, self.sent = send_sem, recv_sem, 0, []
        self.y_idx = lax.axis_index("yax")
        self.x_idx = lax.axis_index("xax")
        self.z, self.y = self.y_idx // NY, self.y_idx % NY
        self.chip, self.core = self.x_idx // 2, self.x_idx % 2

    def at_plane(self, dz, dy):
        return {"yax": (self.z + dz) % NZ * NY + (self.y + dy) % NY, "xax": self.x_idx}

    def at_line(self, dx, other_core):
        core = 1 - self.core if other_core else self.core
        return {"yax": self.y_idx, "xax": (self.chip + dx) % NX * 2 + core}

    def send(self, src, dst, where):
        copy = pltpu.make_async_remote_copy(
            src_ref=src, dst_ref=dst, send_sem=self.send_sem.at[self.count], recv_sem=self.recv_sem.at[self.count],
            device_id=where, device_id_type=MESH_ID)
        self.count += 1
        copy.start()
        self.sent.append(copy)
        return copy

    def finish(self):
        for copy in self.sent:
            copy.wait_send()
        self.sent = []

    def barrier(self):
        barrier = pltpu.get_barrier_semaphore()
        peers = [self.at_line(dx, oc) for dx in range(NX) for oc in (0, 1) if (dx, oc) != (0, 0)]
        peers += [self.at_plane(dz, dy) for dz in range(NZ) for dy in range(NY) if (dz, dy) != (0, 0)]
        for peer in peers:
            pl.semaphore_signal(barrier, inc=1, device_id=peer, device_id_type=MESH_ID)
        pl.semaphore_wait(barrier, len(peers))


def plane_gather(links, buf):
    cols = buf.shape[-1]
    parts = []
    for part in range(2):
        lo = part * (cols // 2)
        mid = lo + cols // 4
        hi = lo + cols // 2

        def slot(du, dv, a, b, half=0, part=part):
            dz, dy = (dv, du) if part == 0 else (du, dv)
            return buf.at[half, (links.z + dz) % NZ, (links.y + dy) % NY, :, pl.ds(a, b - a)]

        def node(du, dv, part=part):
            return links.at_plane(dv, du) if part == 0 else links.at_plane(du, dv)

        parts.append((lo, mid, hi, slot, node))

    partner = links.at_line(0, True)
    crossing = []

    def give(p, du, dv):
        lo, mid, hi, slot, node = p
        crossing.append(links.send(slot(du, dv, lo, hi), slot(du, dv, lo, hi, half=1), partner))

    def push(p, du, dv, to_u, to_v, a=None, b=None):
        lo, mid, hi, slot, node = p
        a, b = (lo if a is None else a), (hi if b is None else b)
        return links.send(slot(du, dv, a, b), slot(du, dv, a, b), node(to_u, to_v))

    state = []
    for p in parts:
        s = {"u+": push(p, 0, 0, 1, 0), "u-": push(p, 0, 0, -1, 0)}
        s["v+", 0] = push(p, 0, 0, 0, 1)
        s["v-", 0] = push(p, 0, 0, 0, -1)
        state.append(s)
    for p in parts:
        give(p, 0, 0)
    for p, s in zip(parts, state):
        s["u+"].wait_recv()
        s["ur+"] = push(p, -1, 0, 1, 0, p[0], p[1])
        s["v+", 1] = push(p, -1, 0, 0, 1)
        s["v-", 1] = push(p, -1, 0, 0, -1)
        give(p, -1, 0)
    for p, s in zip(parts, state):
        s["u-"].wait_recv()
        s["ur-"] = push(p, 1, 0, -1, 0, p[1], p[2])
        s["v+", 2] = push(p, 1, 0, 0, 1)
        s["v-", 2] = push(p, 1, 0, 0, -1)
        give(p, 1, 0)
    offset = {0: 0, 1: -1, 2: 1, 3: 2}

    def arrive(p, s, k):
        s["v+", k].wait_recv()
        if k in (0, 3):
            s["vr+", k] = push(p, offset[k], -1, 0, 1)
        give(p, offset[k], -1)
        s["v-", k].wait_recv()
        if k in (1, 2):
            s["vr-", k] = push(p, offset[k], 1, 0, -1)
        give(p, offset[k], 1)

    for p, s in zip(parts, state):
        arrive(p, s, 0)
    for p, s in zip(parts, state):
        s["ur+"].wait_recv()
        s["ur-"].wait_recv()
        s["v+", 3] = push(p, 2, 0, 0, 1)
        s["v-", 3] = push(p, 2, 0, 0, -1)
        give(p, 2, 0)
    for k in (1, 2, 3):
        for p, s in zip(parts, state):
            arrive(p, s, k)
    for k, name in ((0, "vr+"), (1, "vr-"), (2, "vr-"), (3, "vr+")):
        for p, s in zip(parts, state):
            s[name, k].wait_recv()
            give(p, offset[k], 2)
    return crossing


def eye_mask():
    return lax.broadcasted_iota(jnp.int32, (128, 128), 0) == lax.broadcasted_iota(jnp.int32, (128, 128), 1)


def norm_gather(links, rows_f32, gain_ref, xbuf, stat, out):
    rows, chunk = rows_f32.shape
    xbuf[0, :rows, :] = rows_f32
    xbuf[0, rows:, :] = jnp.broadcast_to(gain_ref[...], (8, chunk))
    line = [links.send(xbuf.at[0], xbuf.at[(NX - dx) % NX], links.at_line(dx, 0)) for dx in (1, 3, 2)]
    yield
    for c in line:
        c.wait_recv()
    held = xbuf[:, :rows, :]
    count = NX * chunk
    mean = jnp.sum(jnp.sum(held, axis=0), axis=-1, keepdims=True) / count
    dev = held - mean[None]
    square = jnp.sum(jnp.sum(dev * dev, axis=0), axis=-1, keepdims=True)
    lane = lax.broadcasted_iota(jnp.int32, (rows, 128), 1)
    stat[0] = jnp.where(lane == 0, mean, square)
    links.send(stat.at[0], stat.at[1], links.at_line(0, True)).wait_recv()
    other_mean, other_square = stat[1, :, 0:1], stat[1, :, 1:2]
    both = (mean + other_mean) * 0.5
    gap = mean - other_mean
    var = (square + other_square + gap * gap * (count * 0.5)) / (2 * count)
    scale = lax.rsqrt(var + EPS)
    for e in range(NX):
        out[0, links.z, links.y, :, e * chunk:(e + 1) * chunk] = (
            (xbuf[e, :rows, :] - both) * scale * xbuf[e, rows:rows + 1, :]).astype(jnp.bfloat16)
    for c in plane_gather(links, out):
        c.wait_recv()


def step_kernel(vocab_own, own_rows, hid_ref, gain_a, gain_f, cos_ref, sin_ref, len_ref, k_hbm, v_hbm,
                wq_ref, wk_ref, wv_ref, wg_ref, wu_ref, wo_hbm, wd_hbm, emb_ref,
                knew_ref, vnew_ref, z_ref, norm_ref,
                k_buf, v_buf, wo_buf, wd_buf, n_buf, w_buf, wq_t, wq_buf, sel, sel_t, qx, qr, qy, qf,
                kvp, kvr, o_buf, o_got, o_send, o_all, act,
                part, ra1, rb1, ra2, rb2, acc_a, acc_b, xbuf, stat, xbuf2, stat2, f_buf, emb_buf, lse_x, lse_y,
                send_sem, recv_sem, local_sem):
    links = Links(send_sem, recv_sem)
    f32, bf16 = jnp.float32, jnp.bfloat16
    z, y, xid, yid = links.z, links.y, links.x_idx, links.y_idx
    rows, chunk = hid_ref.shape[2], hid_ref.shape[3]
    half = chunk // 2
    nx2, nyz = 2 * NX, NY * NZ
    group = NY * rows
    head = 128
    pad = 8
    others = [(dx, oc) for dx, oc in ((0, 1), (1, 0), (3, 0), (1, 1), (3, 1), (2, 0), (2, 1))]

    def line_id(dx, oc):
        core = 1 - links.core if oc else links.core
        return (links.chip + dx) % NX * 2 + core

    local = []

    def fetch(src, dst):
        copy = pltpu.make_async_copy(src, dst, local_sem.at[len(local)])
        copy.start()
        local.append(copy)
        return copy

    ff = wg_ref.shape[1] // nx2

    def w_piece(ref, dx, oc):
        return ref.at[:, pl.ds(pl.multiple_of(line_id(dx, oc) * ff, ff), ff)]

    def w_slot(which, dx, oc):
        back = (NX - dx) % NX
        return w_buf.at[int(oc), pl.ds(back * chunk, chunk), pl.ds(which * ff, ff)]

    take = emb_buf.shape[1]

    def emb_start(xi):
        return pl.multiple_of(vocab_own * xi // 16 * 16 - xi // (nx2 - 1) * 16, 16)

    def emb_piece(dx, oc):
        return emb_ref.at[pl.ds(emb_start(line_id(dx, oc)), take), :]

    def emb_slot(dx, oc):
        return emb_buf.at[int(oc), :, pl.ds((NX - dx) % NX * chunk, chunk)]

    own_w = [fetch(w_piece(wg_ref, 0, 0), w_slot(0, 0, 0)), fetch(w_piece(wu_ref, 0, 0), w_slot(1, 0, 0))]
    got_kv = [fetch(k_hbm, k_buf), fetch(v_hbm, v_buf)]
    got_wo, got_wd = fetch(wo_hbm, wo_buf), fetch(wd_hbm, wd_buf)
    own_emb = fetch(emb_piece(0, 0), emb_slot(0, 0))

    qc = wq_ref.shape[1]
    qs = qc // nx2
    per = head // qs
    eye_q = (lax.broadcasted_iota(jnp.int32, (qc, qc), 0) == lax.broadcasted_iota(jnp.int32, (qc, qc), 1))
    wq_t[...] = lax.dot_general(eye_q.astype(bf16), wq_ref[...], (((1,), (1,)), ((), ())),
                                preferred_element_type=f32).astype(bf16)
    wq_buf[...] = jnp.zeros(wq_buf.shape, bf16)

    def q_rows(xi):
        return pl.ds(pl.multiple_of(xi % per * qs, qs), qs)

    wq_buf[0, q_rows(xid), 0:chunk] = wq_t[pl.ds(pl.multiple_of(xid * qs, qs), qs), :]
    links.barrier()

    front = norm_gather(links, hid_ref[z, y].astype(f32), gain_a, xbuf, stat, n_buf)
    next(front)
    wq_got, w_got = [], []
    for dx, oc in others:
        xi = line_id(dx, oc)
        wq_got.append(links.send(wq_t.at[pl.ds(pl.multiple_of(xi * qs, qs), qs), :],
                                 wq_buf.at[int(oc), q_rows(xi), pl.ds((NX - dx) % NX * chunk, chunk)],
                                 links.at_line(dx, oc)))
    for dx, oc in others:
        for which, ref in enumerate((wg_ref, wu_ref)):
            w_got.append(links.send(w_piece(ref, dx, oc), w_slot(which, dx, oc), links.at_line(dx, oc)))

    total_rows = nyz * rows
    r_id = lax.broadcasted_iota(jnp.int32, (nx2 * nyz * pad, 1), 0)
    r_j = r_id % pad
    r_src = jnp.where(r_j < own_rows, r_id // pad % nyz * rows + r_id // (pad * nyz) * own_rows + r_j, -1)
    s_id = lax.broadcasted_iota(jnp.int32, (1, total_rows), 1)
    sel[...] = jnp.where(r_src == s_id, 1.0, 0.0).astype(bf16)
    t_id = lax.broadcasted_iota(jnp.int32, (total_rows, 1), 0)
    t_in = t_id % rows
    t_src = t_in // own_rows * (nyz * pad) + t_id // rows * pad + t_in % own_rows
    u_id = lax.broadcasted_iota(jnp.int32, (1, nx2 * nyz * pad), 1)
    sel_t[...] = jnp.where(t_src == u_id, 1.0, 0.0).astype(bf16)
    k_id = lax.broadcasted_iota(jnp.int32, (nx2 * pad, rows), 0)
    k_src = jnp.where(k_id % pad < own_rows, k_id // pad * own_rows + k_id % pad, -1)
    sel_kv = jnp.where(k_src == lax.broadcasted_iota(jnp.int32, (nx2 * pad, rows), 1), 1.0, 0.0).astype(bf16)

    for _ in front:
        pass

    n_own = jnp.dot(sel_kv, n_buf[0, z, y, :, 0:chunk], preferred_element_type=f32).astype(bf16)
    kvp[:, :, :head] = jnp.dot(n_own, wk_ref[...], preferred_element_type=f32).reshape(nx2, pad, head)
    kvp[:, :, head:] = jnp.dot(n_own, wv_ref[...], preferred_element_type=f32).reshape(nx2, pad, head)
    kv_got = [links.send(kvp.at[line_id(dx, oc)], kvr.at[xid], links.at_line(dx, oc)) for dx, oc in others]
    kvr[xid] = kvp[xid]

    for c in wq_got:
        c.wait_recv()

    def wide(buf, i, h):
        return buf[h, i].reshape(group, NX * chunk)

    q_blocks = []
    for i in range(NZ):
        q_blocks.append((lax.dot_general(wide(n_buf, i, 0), wq_buf[0], (((1,), (1,)), ((), ())), preferred_element_type=f32)
                         + lax.dot_general(wide(n_buf, i, 1), wq_buf[1], (((1,), (1,)), ((), ())), preferred_element_type=f32)
                         ).astype(bf16))
    q_all = jnp.concatenate(q_blocks, axis=0)
    span = nyz * pad
    for i in range(nx2):
        qx[i] = jnp.dot(sel[i * span:(i + 1) * span, :], q_all, preferred_element_type=f32).astype(bf16)
    q_got = [links.send(qx.at[line_id(dx, oc)], qr.at[xid], links.at_line(dx, oc)) for dx, oc in others]
    qr[xid] = qx[xid]
    for c in q_got:
        c.wait_recv()
    for j in range(qc // head):
        piece = qr[j * per].astype(f32)
        for i in range(1, per):
            piece = piece + qr[j * per + i].astype(f32)
        qy[:, :, j * head:(j + 1) * head] = piece.reshape(nyz, pad, head)
    plane = [(dz, dy) for dz in range(NZ) for dy in range(NY) if (dz, dy) != (0, 0)]

    def plane_id(dz, dy):
        return (z + dz) % NZ * NY + (y + dy) % NY

    y_got = [links.send(qy.at[plane_id(dz, dy)], qf.at[yid], links.at_plane(dz, dy)) for dz, dy in plane]
    qf[yid] = qy[yid]

    for c in kv_got:
        c.wait_recv()
    kv_sum = kvr[0]
    for i in range(1, nx2):
        kv_sum = kv_sum + kvr[i]
    kv_new = kv_sum.astype(bf16).astype(f32)

    def turn(v, b=None):
        cos, sin = (cos_ref[...], sin_ref[...]) if b is None else (cos_ref[b:b + 1, :], sin_ref[b:b + 1, :])
        return (v * cos + pltpu.roll(v, head // 2, 1) * sin).astype(bf16)

    k_new = turn(kv_new[:, :head])
    knew_ref[...] = k_new
    vnew_ref[...] = kv_new[:, head:].astype(bf16)
    k_row, v_row = k_new.astype(f32), kv_new[:, head:]
    for c in got_kv:
        c.wait()
    for c in y_got:
        c.wait_recv()
    seq = k_buf.shape[1]
    score_scale = head ** -0.5
    position = lax.broadcasted_iota(jnp.int32, (1, seq), 1)
    o_buf[...] = jnp.zeros(o_buf.shape, f32)
    for b in range(own_rows):
        q_b = jnp.concatenate([turn(qf[:, b, j * head:(j + 1) * head], b) for j in range(qc // head)], axis=0)
        scores = lax.dot_general(q_b, k_buf[b], (((1,), (1,)), ((), ())), preferred_element_type=f32) * score_scale
        score_new = jnp.sum(q_b.astype(f32) * k_row[b:b + 1, :], axis=-1, keepdims=True) * score_scale
        valid = position < len_ref[b:b + 1, 0:1]
        top = jnp.maximum(jnp.max(jnp.where(valid, scores, -jnp.inf), axis=-1, keepdims=True), score_new)
        weights = jnp.where(valid, jnp.exp(scores - top), 0.0)
        weight_new = jnp.exp(score_new - top)
        denom = jnp.sum(weights, axis=-1, keepdims=True) + weight_new
        o_b = jnp.dot((weights / denom).astype(bf16), v_buf[b], preferred_element_type=f32)
        o_b = o_b + (weight_new / denom).astype(bf16).astype(f32) * v_row[b:b + 1, :]
        o_b = o_b.astype(bf16).astype(f32)
        for j in range(qc // head):
            o_buf[:, b, j * head:(j + 1) * head] = o_b[j * nyz:(j + 1) * nyz, :]
    o_back = [links.send(o_buf.at[plane_id(dz, dy)], o_got.at[yid], links.at_plane(dz, dy)) for dz, dy in plane]
    o_got[yid] = o_buf[yid]
    for c in o_back:
        c.wait_recv()
    o_all[xid] = o_got[...].reshape(span, qc).astype(bf16)
    o_line = [links.send(o_all.at[xid], o_all.at[xid], links.at_line(dx, oc)) for dx, oc in others]

    for c in own_w:
        c.wait()
    for c in w_got:
        c.wait_recv()
    own_cols = pl.ds(pl.multiple_of(xid * ff, ff), ff)
    a_got = []
    partner = links.at_line(0, True)
    for i in range(NZ):
        both = (jnp.dot(wide(n_buf, i, 0), w_buf[0], preferred_element_type=f32)
                + jnp.dot(wide(n_buf, i, 1), w_buf[1], preferred_element_type=f32)).astype(bf16).astype(f32)
        gate, up = both[:, :ff], both[:, ff:]
        act[i, :, own_cols] = (gate * jax.nn.sigmoid(gate) * up).astype(bf16)
        here = act.at[i, :, own_cols]
        a_got.append([links.send(here, here, links.at_line(dx, 0)) for dx in (1, 3, 2)]
                     + [links.send(here, here, partner)])

    emb = [links.send(emb_piece(dx, oc), emb_slot(dx, oc), links.at_line(dx, oc)) for dx, oc in others[:5]]

    for c in o_line:
        c.wait_recv()
    got_wo.wait()
    got_wd.wait()
    for i in range(NZ):
        o_nat = jnp.dot(sel_t[i * group:(i + 1) * group, :], o_all[...].reshape(nx2 * span, qc),
                        preferred_element_type=f32).astype(bf16)
        part[i] = jnp.dot(o_nat, wo_buf[...], preferred_element_type=f32).reshape(NY, rows, chunk)
    passed = []
    for i in range(NZ):
        for dx, c in zip((1, 3, 2), a_got[i]):
            c.wait_recv()
            came = pl.ds(pl.multiple_of(line_id((NX - dx) % NX, 0) * ff, ff), ff)
            passed.append(links.send(act.at[i, :, came], act.at[i, :, came], partner))
        a_got[i][3].wait_recv()
    for i in range(NZ):
        for c in passed[i * 3:i * 3 + 3]:
            c.wait_recv()
        part[i] = part[i] + jnp.dot(act[i], wd_buf[...], preferred_element_type=f32).reshape(NY, rows, chunk)

    low, high = pl.ds(0, half), pl.ds(half, half)
    first = []
    for d in (1, 3, 2):
        first.append((
            links.send(part.at[:, (y + d) % NY, :, low], ra1.at[d - 1], links.at_plane(0, d)),
            links.send(part.at[(z + d) % NZ, :, :, high], rb1.at[d - 1], links.at_plane(d, 0))))
    for ca, cb in first:
        ca.wait_recv()
        cb.wait_recv()
    acc_a[...] = (part[:, y, :, :half] + ra1[0]) + (ra1[1] + ra1[2])
    second_a = [links.send(acc_a.at[(z + d) % NZ], ra2.at[d - 1], links.at_plane(d, 0)) for d in (1, 3, 2)]
    acc_b[...] = (part[z, :, :, half:] + rb1[0]) + (rb1[1] + rb1[2])
    second_b = [links.send(acc_b.at[(y + d) % NY], rb2.at[d - 1], links.at_plane(0, d)) for d in (1, 3, 2)]
    for c in second_a + second_b:
        c.wait_recv()
    branch = jnp.concatenate([(acc_a[z] + ra2[0]) + (ra2[1] + ra2[2]), (acc_b[y] + rb2[0]) + (rb2[1] + rb2[2])], axis=1)
    back = norm_gather(links, hid_ref[z, y].astype(f32) + branch, gain_f, xbuf2, stat2, f_buf)
    next(back)
    emb += [links.send(emb_piece(dx, oc), emb_slot(dx, oc), links.at_line(dx, oc)) for dx, oc in others[5:]]
    for _ in back:
        pass
    own_emb.wait()
    for c in emb:
        c.wait_recv()

    for i in range(NZ):
        z_ref[i * group:(i + 1) * group, :] = (
            lax.dot_general(wide(f_buf, i, 0), emb_buf[0], (((1,), (1,)), ((), ())), preferred_element_type=f32)
            + lax.dot_general(wide(f_buf, i, 1), emb_buf[1], (((1,), (1,)), ((), ())), preferred_element_type=f32))

    shift = vocab_own * xid - emb_start(xid)
    eye = lax.broadcasted_iota(jnp.int32, (128, 128), 0) == lax.broadcasted_iota(jnp.int32, (128, 128), 1)
    col = lax.broadcasted_iota(jnp.int32, (128, take), 1)
    own = (col >= shift) & (col < shift + vocab_own)
    blocks = z_ref.shape[0] // 128
    for b in range(blocks):
        zb = jnp.where(own, z_ref[b * 128:(b + 1) * 128, :], -jnp.inf)
        top = jnp.max(zb, axis=1, keepdims=True)
        mass = jnp.sum(jnp.exp(zb - top), axis=1, keepdims=True)
        lse_x[xid, b:b + 1, :] = jnp.sum(jnp.where(eye, top, 0.0), axis=0, keepdims=True)
        lse_x[xid, 8 + b:9 + b, :] = jnp.sum(jnp.where(eye, mass, 0.0), axis=0, keepdims=True)
    for b in range(blocks, 8):
        lse_x[xid, b:b + 1, :] = jnp.zeros((1, 128), f32)
        lse_x[xid, 8 + b:9 + b, :] = jnp.ones((1, 128), f32)

    def merge(ref):
        tops = ref[:, :8, :]
        top = jnp.max(tops, axis=0)
        return top, jnp.sum(ref[:, 8:, :] * jnp.exp(tops - top[None]), axis=0)

    got = [links.send(lse_x.at[xid], lse_x.at[xid], links.at_line(dx, oc)) for dx, oc in others]
    for c in got:
        c.wait_recv()
    top, mass = merge(lse_x)
    lse_y[yid, :8, :] = top
    lse_y[yid, 8:, :] = mass
    got = [links.send(lse_y.at[yid], lse_y.at[yid], links.at_plane(dz, dy)) for dz, dy in plane]
    for c in got:
        c.wait_recv()
    top, mass = merge(lse_y)
    norm_ref[...] = top + jnp.log(mass)
    links.finish()


def whole_step(hidden, cos, sin, lens, k_cache, v_cache, g_attn, w_query, w_key, w_value,
               w_gate, w_up, w_out, w_down, g_final, embedding):
    total_rows, chunk = hidden.shape
    own_rows, seq, head = k_cache.shape
    rows = total_rows // (NY * NZ)
    vocab_own = embedding.shape[0] // (2 * NX)
    take = (vocab_own + 30) // 16 * 16
    half = chunk // 2
    qc = w_query.shape[1]
    ff = w_gate.shape[1] // (2 * NX)
    f32, bf16 = jnp.float32, jnp.bfloat16
    nyz, nx2, pad = NY * NZ, 2 * NX, 8
    copies = 360
    vmem = pl.BlockSpec(memory_space=pltpu.VMEM)
    hbm = pl.BlockSpec(memory_space=pl.ANY)
    V = pltpu.VMEM
    return pl.pallas_call(
        lambda *refs: step_kernel(vocab_own, own_rows, *refs),
        out_shape=(jax.ShapeDtypeStruct((pad, head), bf16), jax.ShapeDtypeStruct((pad, head), bf16),
                   jax.ShapeDtypeStruct((total_rows, take), f32), jax.ShapeDtypeStruct((8, 128), f32)),
        in_specs=[vmem] * 6 + [hbm] * 2 + [vmem] * 3 + [hbm] * 5,
        out_specs=(vmem,) * 4,
        scratch_shapes=[
            V((own_rows, seq, head), bf16), V((own_rows, seq, head), bf16), V((qc, chunk), bf16),
            V((nx2 * ff, chunk), bf16), V((2, NZ, NY, rows, NX * chunk), bf16), V((2, NX * chunk, 2 * ff), bf16),
            V((qc, chunk), bf16), V((2, head, NX * chunk), bf16),
            V((nx2 * nyz * pad, total_rows), bf16), V((total_rows, nx2 * nyz * pad), bf16),
            V((nx2, nyz * pad, head), bf16), V((nx2, nyz * pad, head), bf16),
            V((nyz, pad, qc), f32), V((nyz, pad, qc), f32),
            V((nx2, pad, 2 * head), f32), V((nx2, pad, 2 * head), f32),
            V((nyz, pad, qc), f32), V((nyz, pad, qc), f32), V((8, 128), f32), V((nx2, nyz * pad, qc), bf16),
            V((NZ, NY * rows, nx2 * ff), bf16),
            V((NZ, NY, rows, chunk), f32),
            V((3, NZ, rows, half), f32), V((3, NY, rows, half), f32), V((3, rows, half), f32), V((3, rows, half), f32),
            V((NZ, rows, half), f32), V((NY, rows, half), f32),
            V((NX, rows + 8, chunk), f32), V((2, rows, 128), f32), V((NX, rows + 8, chunk), f32), V((2, rows, 128), f32),
            V((2, NZ, NY, rows, NX * chunk), bf16), V((2, take, NX * chunk), bf16),
            V((nx2, 16, 128), f32), V((nyz, 16, 128), f32),
            pltpu.SemaphoreType.DMA((copies,)), pltpu.SemaphoreType.DMA((copies,)), pltpu.SemaphoreType.DMA((8,)),
        ],
        compiler_params=pltpu.CompilerParams(
            collective_id=1, has_side_effects=True, vmem_limit_bytes=60 * 1024 * 1024),
        name="decode_step",
    )(hidden.reshape(NZ, NY, rows, chunk), g_attn[None, :], g_final[None, :], cos, sin, lens, k_cache, v_cache,
      w_query, w_key, w_value, w_gate, w_up, w_out, w_down, embedding)


def solution(mesh):
    x_size = mesh.shape["xax"]
    row_spec = P(("dp", "yax", "xax"))

    def local_step(hidden, cache_len, k_cache, v_cache, g_attn, w_query, w_key, w_value,
                   w_gate, w_up, w_out, w_down, g_final, embedding):
        rows = hidden.shape[0]
        own_rows, _, head_dim = k_cache.shape
        y_idx = lax.axis_index("yax")
        x_idx = lax.axis_index("xax")
        own_start = (y_idx * x_size + x_idx) * own_rows
        len_own = jnp.pad(lax.dynamic_slice_in_dim(cache_len, own_start, own_rows, axis=0), (0, 8 - own_rows))
        angles = rope_angle(len_own, head_dim)
        cos_half, sin_half = jnp.cos(angles), jnp.sin(angles)
        cos = jnp.concatenate([cos_half, cos_half], axis=1)
        sin = jnp.concatenate([-sin_half, sin_half], axis=1)
        lens = jnp.broadcast_to(len_own[:, None], (8, 128))
        key_own, value_own, logits_wide, norm_tile = whole_step(
            hidden, cos, sin, lens, k_cache, v_cache, g_attn, w_query, w_key, w_value,
            w_gate, w_up, w_out, w_down, g_final, embedding)
        vocab_own = embedding.shape[0] // x_size
        log_norm = norm_tile[:rows // 128].reshape(rows)
        shift = vocab_own * x_idx - (vocab_own * x_idx // 16 * 16 - x_idx // (x_size - 1) * 16)
        logits = lax.dynamic_slice_in_dim(logits_wide, shift, vocab_own, axis=1)
        return key_own[:own_rows], value_own[:own_rows], logits - log_norm[:, None], log_norm

    in_specs = (P("dp", "xax"), P("dp"), row_spec, row_spec, P("xax"), P("xax", "yax"),
                P("xax", None), P("xax", None), P("xax", "yax"), P("xax", "yax"),
                P("yax", "xax"), P("yax", "xax"), P("xax"), P("yax", "xax"))
    out_specs = (row_spec, row_spec, P("dp", ("yax", "xax")), P("dp"))
    return jax.shard_map(local_step, mesh=mesh, in_specs=in_specs, out_specs=out_specs, check_vma=False)
```

time: 265 us -> 174 us (0.66)
  blocking collectives: 116 us -> 0 us
  Pallas kernels: 87.3 us -> 166 us
  matrix products: 17.6 us -> 0 us
  waiting for transfers between devices: 13.3 us -> 0 us
  starting transfers between devices: 11.7 us -> 0 us
  other arithmetic: 13.1 us -> 2.78 us
    psum x2 -> x0, blocking collectives: 101 us -> none  [the longest x1 87.1 us: local_step(): projected = lax.psum(proj_part, 'xax').astype(jnp.bfloat16)]
    pallas_call x1, Pallas kernels: 87.3 us -> 166 us  [whole_step(): pl.pallas_call(lambda *refs: step_kernel(vocab_own, own_rows, *refs), out...]
    dot_general x10 -> x0, matrix products: 17.6 us -> none  [the longest x1 3.24 us: local_step(): jnp.dot(mlp_act, w_down, preferred_element_type=jnp.float32)]
    all_gather x1 -> x0, blocking collectives: 15.4 us -> none  [local_step(): attn_grp = lax.all_gather(attn_own, 'xax', axis=0, tiled=True)]
    all_to_all x2 -> x0, waiting for transfers between devices: 13.3 us -> none  [the longest x1 6.75 us: local_step(): query_grp = lax.all_to_all(query, 'yax', 0, 1, tiled=True)]
    all_to_all x2 -> x0, starting transfers between devices: 11.7 us -> none  [the longest x1 7.77 us: local_step(): query_grp = lax.all_to_all(query, 'yax', 0, 1, tiled=True)]
  transfers between devices with their start and end apart: 2 -> 0, of which waited for: 2 -> 0; matrix products, arithmetic and copies ran while one was open for 2% -> 0% of each run, Pallas kernels for 0% -> 0%
where the time goes in v2:
time: 174 us
  Pallas kernels  166 us (95%)
  local copies, waits for them, and re-layouts  4.75 us (3%)
  other arithmetic  2.78 us (2%)
    pallas_call x1, Pallas kernels, whole_step(): pl.pallas_call(lambda *refs: step_kernel(vocab_own, own_rows, *refs), out...  166 us

profile of v2, /device:TPU:1, one launch (start us, length us, event | category | flops | bytes accessed | tf_op | source)
XLA Modules:
  0.0 173.8 jit_solution(459376089505667022)
XLA Ops:
  0.7 0.8 dynamic_slice.6
  1.5 0.7 broadcast_in_dim.16.refs_5_
  2.1 0.1 fusion
  2.2 0.7 pad_maximum_fusion
  2.9 165.5 %decode_step.1 = (bf16[8,128]{1,0:T(8,128)(2,1)}, bf16[8,128]{1,0:T(8,128)(2,1)}, f32[768,416]{1,0:T(8,128)}, f32[8,128]{1,0:T(8,128)}) custom-call(bf16[4,4,48,512]{3,2,1,0:T(8,128)(2,1)} %bitcast.7, f32[1,512]{1,0:T(1,128)} %bitcast.10, f32[1,512]{1,0:T(1,128)} %bitcast.11, f32[8,128]{1,0:T(8,128)} %get-tuple-element.21.refs_3_, ...), custom_call_target="tpu_custom_call" | custom-call | tf_op jit(solution)/shard_map/decode_step/pallas_call | solution.py:468
  168.5 0.7 slice_bitcast_fusion
  169.1 0.0 copy-start
  169.1 2.0 %dynamic-slice_subtract_fusion = f32[768,394]{1,0:T(8,128)S(1)} fusion(f32[768,416]{1,0:T(8,128)} %get-tuple-element.10, s32[]{:T(128)S(6)} %select_n.17, f32[768]{0:T(1024)S(1)} %slice_bitcast_fusion), kind=kLoop, calls=%fused_computation | loop fusion | flops 302592 | bytes 2423812 | tf_op jit(solution)/shard_map/sub | solution.py:523
  171.1 0.0 copy-done
  171.1 0.0 copy-start.2
  171.2 0.0 copy-start.1
  171.2 1.5 copy.18
  172.6 0.0 copy-done.2
  172.6 0.6 copy.21
  173.2 0.0 copy-done.1
  173.2 0.6 copy.22
  (2 shorter events, 0.0 us)
Async XLA Ops:
  169.1 2.0 %copy-start = (f32[768]{0:T(1024)}, f32[768]{0:T(1024)S(1)}, u32[]{:S(2)}) copy-start(f32[768]{0:T(1024)S(1)} %slice_bitcast_fusion) | copy-start | bytes 9220
  171.1 1.5 copy-start.2
  171.2 2.1 %copy-start.1 = (bf16[8,128]{1,0:T(8,128)(2,1)S(1)}, bf16[8,128]{1,0:T(8,128)(2,1)}, u32[]{:S(2)}) copy-start(bf16[8,128]{1,0:T(8,128)(2,1)} %get-tuple-element.9) | copy-start | bytes 6148

commit v3 on v2

--- a/solution.py
+++ b/solution.py
@@ -15,6 +15,21 @@
     half_dim = head_dim // 2
     inv_freq = ROPE_BASE ** (-(jnp.arange(half_dim, dtype=jnp.float32) * 2.0) / head_dim)
     return positions.astype(jnp.float32)[:, None] * inv_freq[None, :]
+
+
+class Phases:
+    def __init__(self):
+        self.open = None
+
+    def __call__(self, name):
+        self.close()
+        self.open = jax.named_scope(name)
+        self.open.__enter__()
+
+    def close(self):
+        if self.open is not None:
+            self.open.__exit__(None, None, None)
+        self.open = None
 
 
 class Links:
@@ -27,6 +42,10 @@
 
     def at_plane(self, dz, dy):
         return {"yax": (self.z + dz) % NZ * NY + (self.y + dy) % NY, "xax": self.x_idx}
+
+    def slot_rows(self, dz, dy, rows):
+        slot = (self.z + dz) % NZ * NY + (self.y + dy) % NY
+        return pl.ds(pl.multiple_of(slot * rows, rows), rows)
 
     def at_line(self, dx, other_core):
         core = 1 - self.core if other_core else self.core
@@ -57,6 +76,7 @@
 
 def plane_gather(links, buf):
     cols = buf.shape[-1]
+    rows = buf.shape[1] // (NY * NZ)
     parts = []
     for part in range(2):
         lo = part * (cols // 2)
@@ -65,7 +85,7 @@
 
         def slot(du, dv, a, b, half=0, part=part):
             dz, dy = (dv, du) if part == 0 else (du, dv)
-            return buf.at[half, (links.z + dz) % NZ, (links.y + dy) % NY, :, pl.ds(a, b - a)]
+            return buf.at[half, links.slot_rows(dz, dy, rows), pl.ds(a, b - a)]
 
         def node(du, dv, part=part):
             return links.at_plane(dv, du) if part == 0 else links.at_plane(du, dv)
@@ -134,18 +154,17 @@
     return crossing
 
 
-def eye_mask():
-    return lax.broadcasted_iota(jnp.int32, (128, 128), 0) == lax.broadcasted_iota(jnp.int32, (128, 128), 1)
-
-
 def norm_gather(links, rows_f32, gain_ref, xbuf, stat, out):
     rows, chunk = rows_f32.shape
     xbuf[0, :rows, :] = rows_f32
     xbuf[0, rows:, :] = jnp.broadcast_to(gain_ref[...], (8, chunk))
     line = [links.send(xbuf.at[0], xbuf.at[(NX - dx) % NX], links.at_line(dx, 0)) for dx in (1, 3, 2)]
     yield
+    phase = Phases()
+    phase("ng_line")
     for c in line:
         c.wait_recv()
+    phase("ng_stats")
     held = xbuf[:, :rows, :]
     count = NX * chunk
     mean = jnp.sum(jnp.sum(held, axis=0), axis=-1, keepdims=True) / count
@@ -160,10 +179,14 @@
     var = (square + other_square + gap * gap * (count * 0.5)) / (2 * count)
     scale = lax.rsqrt(var + EPS)
     for e in range(NX):
-        out[0, links.z, links.y, :, e * chunk:(e + 1) * chunk] = (
+        out[0, links.slot_rows(0, 0, rows), e * chunk:(e + 1) * chunk] = (
             (xbuf[e, :rows, :] - both) * scale * xbuf[e, rows:rows + 1, :]).astype(jnp.bfloat16)
-    for c in plane_gather(links, out):
-        c.wait_recv()
+    phase("ng_plane")
+    crossing = plane_gather(links, out)
+    phase("ng_cross")
+    for c in crossing:
+        c.wait_recv()
+    phase.close()
 
 
 def step_kernel(vocab_own, own_rows, hid_ref, gain_a, gain_f, cos_ref, sin_ref, len_ref, k_hbm, v_hbm,
@@ -174,6 +197,7 @@
                 part, ra1, rb1, ra2, rb2, acc_a, acc_b, xbuf, stat, xbuf2, stat2, f_buf, emb_buf, lse_x, lse_y,
                 send_sem, recv_sem, local_sem):
     links = Links(send_sem, recv_sem)
+    phase = Phases()
     f32, bf16 = jnp.float32, jnp.bfloat16
     z, y, xid, yid = links.z, links.y, links.x_idx, links.y_idx
     rows, chunk = hid_ref.shape[2], hid_ref.shape[3]
@@ -216,6 +240,7 @@
     def emb_slot(dx, oc):
         return emb_buf.at[int(oc), :, pl.ds((NX - dx) % NX * chunk, chunk)]
 
+    phase("start")
     own_w = [fetch(w_piece(wg_ref, 0, 0), w_slot(0, 0, 0)), fetch(w_piece(wu_ref, 0, 0), w_slot(1, 0, 0))]
     got_kv = [fetch(k_hbm, k_buf), fetch(v_hbm, v_buf)]
     got_wo, got_wd = fetch(wo_hbm, wo_buf), fetch(wd_hbm, wd_buf)
@@ -233,8 +258,10 @@
         return pl.ds(pl.multiple_of(xi % per * qs, qs), qs)
 
     wq_buf[0, q_rows(xid), 0:chunk] = wq_t[pl.ds(pl.multiple_of(xid * qs, qs), qs), :]
+    phase("barrier")
     links.barrier()
 
+    phase("front_send")
     front = norm_gather(links, hid_ref[z, y].astype(f32), gain_a, xbuf, stat, n_buf)
     next(front)
     wq_got, w_got = [], []
@@ -247,6 +274,7 @@
         for which, ref in enumerate((wg_ref, wu_ref)):
             w_got.append(links.send(w_piece(ref, dx, oc), w_slot(which, dx, oc), links.at_line(dx, oc)))
 
+    phase("selections")
     total_rows = nyz * rows
     r_id = lax.broadcasted_iota(jnp.int32, (nx2 * nyz * pad, 1), 0)
     r_j = r_id % pad
@@ -262,21 +290,25 @@
     k_src = jnp.where(k_id % pad < own_rows, k_id // pad * own_rows + k_id % pad, -1)
     sel_kv = jnp.where(k_src == lax.broadcasted_iota(jnp.int32, (nx2 * pad, rows), 1), 1.0, 0.0).astype(bf16)
 
+    phase.close()
     for _ in front:
         pass
-
-    n_own = jnp.dot(sel_kv, n_buf[0, z, y, :, 0:chunk], preferred_element_type=f32).astype(bf16)
+    phase("kv_part")
+
+    n_own = jnp.dot(sel_kv, n_buf[0, links.slot_rows(0, 0, rows), 0:chunk], preferred_element_type=f32).astype(bf16)
     kvp[:, :, :head] = jnp.dot(n_own, wk_ref[...], preferred_element_type=f32).reshape(nx2, pad, head)
     kvp[:, :, head:] = jnp.dot(n_own, wv_ref[...], preferred_element_type=f32).reshape(nx2, pad, head)
     kv_got = [links.send(kvp.at[line_id(dx, oc)], kvr.at[xid], links.at_line(dx, oc)) for dx, oc in others]
     kvr[xid] = kvp[xid]
 
+    phase("wait_wq")
     for c in wq_got:
         c.wait_recv()
 
     def wide(buf, i, h):
-        return buf[h, i].reshape(group, NX * chunk)
-
+        return buf[h, i * group:(i + 1) * group, :]
+
+    phase("q_mm")
     q_blocks = []
     for i in range(NZ):
         q_blocks.append((lax.dot_general(wide(n_buf, i, 0), wq_buf[0], (((1,), (1,)), ((), ())), preferred_element_type=f32)
@@ -288,8 +320,10 @@
         qx[i] = jnp.dot(sel[i * span:(i + 1) * span, :], q_all, preferred_element_type=f32).astype(bf16)
     q_got = [links.send(qx.at[line_id(dx, oc)], qr.at[xid], links.at_line(dx, oc)) for dx, oc in others]
     qr[xid] = qx[xid]
+    phase("wait_q")
     for c in q_got:
         c.wait_recv()
+    phase("q_sum")
     for j in range(qc // head):
         piece = qr[j * per].astype(f32)
         for i in range(1, per):
@@ -303,6 +337,7 @@
     y_got = [links.send(qy.at[plane_id(dz, dy)], qf.at[yid], links.at_plane(dz, dy)) for dz, dy in plane]
     qf[yid] = qy[yid]
 
+    phase("wait_kv")
     for c in kv_got:
         c.wait_recv()
     kv_sum = kvr[0]
@@ -318,10 +353,12 @@
     knew_ref[...] = k_new
     vnew_ref[...] = kv_new[:, head:].astype(bf16)
     k_row, v_row = k_new.astype(f32), kv_new[:, head:]
+    phase("wait_qy")
     for c in got_kv:
         c.wait()
     for c in y_got:
         c.wait_recv()
+    phase("attention")
     seq = k_buf.shape[1]
     score_scale = head ** -0.5
     position = lax.broadcasted_iota(jnp.int32, (1, seq), 1)
@@ -340,17 +377,21 @@
         o_b = o_b.astype(bf16).astype(f32)
         for j in range(qc // head):
             o_buf[:, b, j * head:(j + 1) * head] = o_b[j * nyz:(j + 1) * nyz, :]
+    phase("wait_oy")
     o_back = [links.send(o_buf.at[plane_id(dz, dy)], o_got.at[yid], links.at_plane(dz, dy)) for dz, dy in plane]
     o_got[yid] = o_buf[yid]
     for c in o_back:
         c.wait_recv()
+    phase("o_send")
     o_all[xid] = o_got[...].reshape(span, qc).astype(bf16)
     o_line = [links.send(o_all.at[xid], o_all.at[xid], links.at_line(dx, oc)) for dx, oc in others]
 
+    phase("wait_w")
     for c in own_w:
         c.wait()
     for c in w_got:
         c.wait_recv()
+    phase("gate_up")
     own_cols = pl.ds(pl.multiple_of(xid * ff, ff), ff)
     a_got = []
     partner = links.at_line(0, True)
@@ -363,16 +404,20 @@
         a_got.append([links.send(here, here, links.at_line(dx, 0)) for dx in (1, 3, 2)]
                      + [links.send(here, here, partner)])
 
+    phase("emb_send")
     emb = [links.send(emb_piece(dx, oc), emb_slot(dx, oc), links.at_line(dx, oc)) for dx, oc in others[:5]]
 
+    phase("wait_o")
     for c in o_line:
         c.wait_recv()
     got_wo.wait()
     got_wd.wait()
+    phase("out_mm")
     for i in range(NZ):
         o_nat = jnp.dot(sel_t[i * group:(i + 1) * group, :], o_all[...].reshape(nx2 * span, qc),
                         preferred_element_type=f32).astype(bf16)
         part[i] = jnp.dot(o_nat, wo_buf[...], preferred_element_type=f32).reshape(NY, rows, chunk)
+    phase("wait_act")
     passed = []
     for i in range(NZ):
         for dx, c in zip((1, 3, 2), a_got[i]):
@@ -380,52 +425,62 @@
             came = pl.ds(pl.multiple_of(line_id((NX - dx) % NX, 0) * ff, ff), ff)
             passed.append(links.send(act.at[i, :, came], act.at[i, :, came], partner))
         a_got[i][3].wait_recv()
+    phase("down_mm")
     for i in range(NZ):
         for c in passed[i * 3:i * 3 + 3]:
             c.wait_recv()
         part[i] = part[i] + jnp.dot(act[i], wd_buf[...], preferred_element_type=f32).reshape(NY, rows, chunk)
 
+    phase("rs_send")
     low, high = pl.ds(0, half), pl.ds(half, half)
     first = []
     for d in (1, 3, 2):
         first.append((
             links.send(part.at[:, (y + d) % NY, :, low], ra1.at[d - 1], links.at_plane(0, d)),
             links.send(part.at[(z + d) % NZ, :, :, high], rb1.at[d - 1], links.at_plane(d, 0))))
+    phase("wait_rs1")
     for ca, cb in first:
         ca.wait_recv()
         cb.wait_recv()
+    phase("rs_sum1")
     acc_a[...] = (part[:, y, :, :half] + ra1[0]) + (ra1[1] + ra1[2])
     second_a = [links.send(acc_a.at[(z + d) % NZ], ra2.at[d - 1], links.at_plane(d, 0)) for d in (1, 3, 2)]
     acc_b[...] = (part[z, :, :, half:] + rb1[0]) + (rb1[1] + rb1[2])
     second_b = [links.send(acc_b.at[(y + d) % NY], rb2.at[d - 1], links.at_plane(0, d)) for d in (1, 3, 2)]
+    phase("wait_rs2")
     for c in second_a + second_b:
         c.wait_recv()
+    phase("rs_sum2")
     branch = jnp.concatenate([(acc_a[z] + ra2[0]) + (ra2[1] + ra2[2]), (acc_b[y] + rb2[0]) + (rb2[1] + rb2[2])], axis=1)
     back = norm_gather(links, hid_ref[z, y].astype(f32) + branch, gain_f, xbuf2, stat2, f_buf)
     next(back)
     emb += [links.send(emb_piece(dx, oc), emb_slot(dx, oc), links.at_line(dx, oc)) for dx, oc in others[5:]]
+    phase.close()
     for _ in back:
         pass
+    phase("wait_emb")
     own_emb.wait()
     for c in emb:
         c.wait_recv()
 
-    for i in range(NZ):
-        z_ref[i * group:(i + 1) * group, :] = (
-            lax.dot_general(wide(f_buf, i, 0), emb_buf[0], (((1,), (1,)), ((), ())), preferred_element_type=f32)
-            + lax.dot_general(wide(f_buf, i, 1), emb_buf[1], (((1,), (1,)), ((), ())), preferred_element_type=f32))
-
+    phase("logits")
+    wide_n = 256
+    for i in range(total_rows // wide_n):
+        cols = slice(i * wide_n, (i + 1) * wide_n)
+        z_ref[:, cols] = (
+            lax.dot_general(emb_buf[0], f_buf[0, cols, :], (((1,), (1,)), ((), ())), preferred_element_type=f32)
+            + lax.dot_general(emb_buf[1], f_buf[1, cols, :], (((1,), (1,)), ((), ())), preferred_element_type=f32))
+
+    phase("lse_own")
     shift = vocab_own * xid - emb_start(xid)
-    eye = lax.broadcasted_iota(jnp.int32, (128, 128), 0) == lax.broadcasted_iota(jnp.int32, (128, 128), 1)
-    col = lax.broadcasted_iota(jnp.int32, (128, take), 1)
-    own = (col >= shift) & (col < shift + vocab_own)
-    blocks = z_ref.shape[0] // 128
+    vid = lax.broadcasted_iota(jnp.int32, (take, 1), 0)
+    own = (vid >= shift) & (vid < shift + vocab_own)
+    blocks = total_rows // 128
     for b in range(blocks):
-        zb = jnp.where(own, z_ref[b * 128:(b + 1) * 128, :], -jnp.inf)
-        top = jnp.max(zb, axis=1, keepdims=True)
-        mass = jnp.sum(jnp.exp(zb - top), axis=1, keepdims=True)
-        lse_x[xid, b:b + 1, :] = jnp.sum(jnp.where(eye, top, 0.0), axis=0, keepdims=True)
-        lse_x[xid, 8 + b:9 + b, :] = jnp.sum(jnp.where(eye, mass, 0.0), axis=0, keepdims=True)
+        zb = jnp.where(own, z_ref[:, b * 128:(b + 1) * 128], -jnp.inf)
+        top = jnp.max(zb, axis=0, keepdims=True)
+        lse_x[xid, b:b + 1, :] = top
+        lse_x[xid, 8 + b:9 + b, :] = jnp.sum(jnp.exp(zb - top), axis=0, keepdims=True)
     for b in range(blocks, 8):
         lse_x[xid, b:b + 1, :] = jnp.zeros((1, 128), f32)
         lse_x[xid, 8 + b:9 + b, :] = jnp.ones((1, 128), f32)
@@ -435,18 +490,22 @@
         top = jnp.max(tops, axis=0)
         return top, jnp.sum(ref[:, 8:, :] * jnp.exp(tops - top[None]), axis=0)
 
+    phase("lse_line")
     got = [links.send(lse_x.at[xid], lse_x.at[xid], links.at_line(dx, oc)) for dx, oc in others]
     for c in got:
         c.wait_recv()
     top, mass = merge(lse_x)
     lse_y[yid, :8, :] = top
     lse_y[yid, 8:, :] = mass
+    phase("lse_plane")
     got = [links.send(lse_y.at[yid], lse_y.at[yid], links.at_plane(dz, dy)) for dz, dy in plane]
     for c in got:
         c.wait_recv()
     top, mass = merge(lse_y)
     norm_ref[...] = top + jnp.log(mass)
+    phase("finish")
     links.finish()
+    phase.close()
 
 
 def whole_step(hidden, cos, sin, lens, k_cache, v_cache, g_attn, w_query, w_key, w_value,
@@ -468,12 +527,12 @@
     return pl.pallas_call(
         lambda *refs: step_kernel(vocab_own, own_rows, *refs),
         out_shape=(jax.ShapeDtypeStruct((pad, head), bf16), jax.ShapeDtypeStruct((pad, head), bf16),
-                   jax.ShapeDtypeStruct((total_rows, take), f32), jax.ShapeDtypeStruct((8, 128), f32)),
+                   jax.ShapeDtypeStruct((take, total_rows), f32), jax.ShapeDtypeStruct((8, 128), f32)),
         in_specs=[vmem] * 6 + [hbm] * 2 + [vmem] * 3 + [hbm] * 5,
         out_specs=(vmem,) * 4,
         scratch_shapes=[
             V((own_rows, seq, head), bf16), V((own_rows, seq, head), bf16), V((qc, chunk), bf16),
-            V((nx2 * ff, chunk), bf16), V((2, NZ, NY, rows, NX * chunk), bf16), V((2, NX * chunk, 2 * ff), bf16),
+            V((nx2 * ff, chunk), bf16), V((2, total_rows, NX * chunk), bf16), V((2, NX * chunk, 2 * ff), bf16),
             V((qc, chunk), bf16), V((2, head, NX * chunk), bf16),
             V((nx2 * nyz * pad, total_rows), bf16), V((total_rows, nx2 * nyz * pad), bf16),
             V((nx2, nyz * pad, head), bf16), V((nx2, nyz * pad, head), bf16),
@@ -485,7 +544,7 @@
             V((3, NZ, rows, half), f32), V((3, NY, rows, half), f32), V((3, rows, half), f32), V((3, rows, half), f32),
             V((NZ, rows, half), f32), V((NY, rows, half), f32),
             V((NX, rows + 8, chunk), f32), V((2, rows, 128), f32), V((NX, rows + 8, chunk), f32), V((2, rows, 128), f32),
-            V((2, NZ, NY, rows, NX * chunk), bf16), V((2, take, NX * chunk), bf16),
+            V((2, total_rows, NX * chunk), bf16), V((2, take, NX * chunk), bf16),
             V((nx2, 16, 128), f32), V((nyz, 16, 128), f32),
             pltpu.SemaphoreType.DMA((copies,)), pltpu.SemaphoreType.DMA((copies,)), pltpu.SemaphoreType.DMA((8,)),
         ],
@@ -519,8 +578,8 @@
         vocab_own = embedding.shape[0] // x_size
         log_norm = norm_tile[:rows // 128].reshape(rows)
         shift = vocab_own * x_idx - (vocab_own * x_idx // 16 * 16 - x_idx // (x_size - 1) * 16)
-        logits = lax.dynamic_slice_in_dim(logits_wide, shift, vocab_own, axis=1)
-        return key_own[:own_rows], value_own[:own_rows], logits - log_norm[:, None], log_norm
+        logits = lax.dynamic_slice_in_dim(logits_wide, shift, vocab_own, axis=0)
+        return key_own[:own_rows], value_own[:own_rows], (logits - log_norm[None, :]).T, log_norm
 
     in_specs = (P("dp", "xax"), P("dp"), row_spec, row_spec, P("xax"), P("xax", "yax"),
                 P("xax", None), P("xax", None), P("xax", "yax"), P("xax", "yax"),

time: 174 us -> 172 us (0.989)
  Pallas kernels: 166 us -> 164 us
    transpose x0 -> x1, other arithmetic: none -> 2.46 us  [local_step(): return (key_own[:own_rows], value_own[:own_rows], (logits - log_norm[None...]
    sub x1 -> x0, other arithmetic: 1.98 us -> none  [local_step(): logits - log_norm[:, None]]
where the time goes in v3:
time: 172 us; the launch traced here: 171 us
  Pallas kernels  164 us (95%)
  local copies, waits for them, and re-layouts  3.28 us (2%)
  other arithmetic  3.26 us (2%)
    pallas_call x1, Pallas kernels, whole_step(): pl.pallas_call(lambda *refs: step_kernel(vocab_own, own_rows, *refs), out...  164 us

profile of v3, /device:TPU:1, one launch (start us, length us, event | category | flops | bytes accessed | tf_op | source)
XLA Modules:
  0.0 171.4 jit_solution(18042165000429350802)
XLA Ops:
  0.7 0.8 dynamic_slice.6
  1.5 0.7 broadcast_in_dim.16.refs_5_
  2.1 0.1 fusion
  2.2 0.7 pad_maximum_fusion
  2.9 164.2 %decode_step.1 = (bf16[8,128]{1,0:T(8,128)(2,1)}, bf16[8,128]{1,0:T(8,128)(2,1)}, f32[416,768]{1,0:T(8,128)}, f32[8,128]{1,0:T(8,128)}) custom-call(bf16[4,4,48,512]{3,2,1,0:T(8,128)(2,1)} %bitcast.9, f32[1,512]{1,0:T(1,128)} %bitcast.12, f32[1,512]{1,0:T(1,128)} %bitcast.13, f32[8,128]{1,0:T(8,128)} %get-tuple-element.17.refs_3_, ...), custom_call_target="tpu_custom_call" | custom-call | tf_op jit(solution)/shard_map/decode_step/pallas_call | solution.py:527
  167.1 0.0 copy-start.2
  167.1 0.0 copy-start.1
  167.1 0.7 slice_bitcast_fusion
  167.8 0.0 copy-start
  167.8 2.5 %subtract_bitcast_fusion = f32[768,394]{0,1:T(8,128)} fusion(f32[416,768]{1,0:T(8,128)} %get-tuple-element.10, s32[]{:T(128)S(6)} %select_n.17, f32[768]{0:T(1024)S(1)} %slice_bitcast_fusion), kind=kLoop, calls=%fused_computation | loop fusion | flops 302592 | bytes 2423812 | tf_op jit(solution)/shard_map/transpose | solution.py:582
  170.2 0.0 copy-done.2
  170.2 0.6 copy.20
  170.8 0.0 copy-done.1
  170.8 0.6 copy.21
  171.4 0.0 copy-done
  (2 shorter events, 0.0 us)
Async XLA Ops:
  167.1 3.2 %copy-start.2 = (bf16[8,128]{1,0:T(8,128)(2,1)S(1)}, bf16[8,128]{1,0:T(8,128)(2,1)}, u32[]{:S(2)}) copy-start(bf16[8,128]{1,0:T(8,128)(2,1)} %get-tuple-element.8) | copy-start | bytes 6148
  167.1 3.7 %copy-start.1 = (bf16[8,128]{1,0:T(8,128)(2,1)S(1)}, bf16[8,128]{1,0:T(8,128)(2,1)}, u32[]{:S(2)}) copy-start(bf16[8,128]{1,0:T(8,128)(2,1)} %get-tuple-element.9) | copy-start | bytes 6148
  167.8 3.6 %copy-start = (f32[768]{0:T(1024)}, f32[768]{0:T(1024)S(1)}, u32[]{:S(2)}) copy-start(f32[768]{0:T(1024)S(1)} %slice_bitcast_fusion) | copy-start | bytes 9220
